TPU v7x, 8 devices: a whole 2x2x1 slice. The times are simulated.
8 devices in a mesh: dp: 8 (over z, y, x, core).
Axes of the slice: x: 2, y: 2, z: 1, core: 2. Of those that a mesh axis runs over, the one named last changes fastest.
Arguments:
- u_norm: bfloat16 [16, 2048, 2048], P(None, 'dp')
- expert_idx: int32 [16, 2048, 8], P(None, 'dp')
- expert_out: bfloat16 [16, 2048, 8, 2048], P(None, 'dp')
- d_out: bfloat16 [16, 2048, 2048], P(None, 'dp')
- w_router: bfloat16 [16, 2048, 64], replicated
Outputs:
- output 1: float32 [], replicated
- output 2: float32 [16, 2048, 64], replicated
- output 3: bfloat16 [16, 2048, 2048], P(None, 'dp')
All inputs are finite; a program needn't handle non-finite values.
Results may differ from a plain program's by a relative error of at most 0.00919422.
Values sent between devices are 32-bit elements.
A program may use at most 1 GiB of HBM per device.

v0:
```python
import jax
import jax.numpy as jnp
from jax import lax
from jax.sharding import PartitionSpec as P

AUX_COEF = 0.02


def router_forward(u_norm, expert_idx, expert_out, d_out, w_router):
    num_exp = w_router.shape[2]
    one_hot = (expert_idx[..., None] == jnp.arange(num_exp)).astype(jnp.float32)
    logits = jnp.einsum('ltd,lde->lte', u_norm, w_router, preferred_element_type=jnp.float32)
    prob_vals = jax.nn.softmax(logits, axis=-1)
    chosen = jnp.sum(one_hot * logits[:, :, None, :], axis=-1)
    gate_vals = jax.nn.softmax(chosen, axis=-1)
    slot_dots = jnp.einsum('ltkd,ltd->ltk', expert_out, d_out, preferred_element_type=jnp.float32)
    return one_hot, prob_vals, gate_vals, slot_dots


def logit_grad(one_hot, prob_vals, gate_vals, slot_dots, aux_pull, loss_scale):
    d_dots = loss_scale * slot_dots
    d_chosen = gate_vals * (d_dots - jnp.sum(gate_vals * d_dots, axis=-1, keepdims=True))
    pull_row = aux_pull[:, None, :]
    aux_grad = prob_vals * (pull_row - jnp.sum(prob_vals * pull_row, axis=-1, keepdims=True))
    return jnp.sum(d_chosen[..., None] * one_hot, axis=2) + aux_grad


def solution(mesh):
    group_size = mesh.shape['dp']

    def local_step(u_norm, expert_idx, expert_out, d_out, w_router):
        num_exp = w_router.shape[2]
        top_k = expert_idx.shape[2]
        tok_all = u_norm.shape[1] * group_size
        one_hot, prob_vals, gate_vals, slot_dots = router_forward(u_norm, expert_idx, expert_out, d_out, w_router)
        local_stats = jnp.concatenate([jnp.sum(one_hot, axis=(1, 2)), jnp.sum(prob_vals, axis=1)], axis=-1)
        glob_stats = lax.psum(local_stats, 'dp')
        exp_frac = glob_stats[:, :num_exp] / (top_k * tok_all)
        prob_mean = glob_stats[:, num_exp:] / tok_all
        aux_total = AUX_COEF * num_exp * jnp.sum(exp_frac * prob_mean)
        main_part = jnp.sum(gate_vals * slot_dots)
        d_logits = logit_grad(one_hot, prob_vals, gate_vals, slot_dots, AUX_COEF * num_exp * exp_frac, float(tok_all))
        d_log16 = d_logits.astype(jnp.bfloat16)
        d_norm = jnp.einsum('lte,lde->ltd', d_log16, w_router, preferred_element_type=jnp.float32).astype(jnp.bfloat16)
        part_grad = jnp.einsum('ltd,lte->lde', u_norm, d_log16, preferred_element_type=jnp.float32)
        d_router = lax.psum(part_grad, 'dp')
        total_loss = lax.psum(main_part, 'dp') + aux_total
        return total_loss, d_router, d_norm

    tok_spec = P(None, 'dp', None)
    return jax.shard_map(local_step, mesh=mesh, in_specs=(tok_spec, tok_spec, P(None, 'dp', None, None), tok_spec, P()), out_specs=(P(), P(), tok_spec), check_vma=False)
```

profile of v0, /device:TPU:0, one launch (start us, length us, event | category | flops | bytes accessed | tf_op | source)
XLA Modules:
  0.0 279.3 jit_solution(9537266995690539949)
XLA Ops:
  7.2 0.0 copy-start
  7.2 0.0 all-reduce.3.cloned.1.call-start
  7.2 10.6 %fusion.31 = f32[16,256,64]{1,2,0:T(8,128)S(1)} fusion(bf16[16,256,2048]{2,1,0:T(8,128)(2,1)} %param.5, bf16[16,2048,64]{1,2,0:T(8,128)(2,1)} %param.9), kind=kOutput, calls=%fused_computation.42 | convolution fusion | flops 1073741824 | bytes 22020096 | tf_op jit(solution)/shard_map/ltd,lde->lte/dot_general | solution.py:12
  17.9 1.4 fusion.30
  19.2 0.0 copy-done
  19.2 2.6 select_reduce_fusion.1
  21.9 1.0 fusion.29
  22.9 82.0 %fusion.4 = f32[16,256,1,8]{3,2,1,0:T(1,128)S(1)} fusion(bf16[16,256,8,2048]{3,2,1,0:T(8,128)(2,1)} %param.7, bf16[16,256,2048,1]{2,1,0,3:T(8,128)(2,1)} %bitcast.19), kind=kOutput, calls=%fused_computation.4 | convolution fusion | flops 134217728 | bytes 151126016 | tf_op jit(solution)/shard_map/ltkd,ltd->ltk/dot_general | solution.py:16
  104.9 1.0 copy.11
  105.9 0.7 multiply_reduce_fusion.1
  106.6 1.7 select_reduce_fusion
  108.3 0.1 pad_maximum_fusion
  108.4 25.4 %all-reduce = (f32[]{:T(128)}, f32[16,128]{1,0:T(8,128)S(1)}) all-reduce(f32[]{:T(128)} %get-tuple-element.4, f32[16,128]{1,0:T(8,128)S(1)} %pad_maximum_fusion), channel_id=1, replica_groups=mesh['dp'=8] {'dp'}, use_global_device_ids=true, to_apply=%region_4.0 | all-reduce | flops 2049 | bytes 16392 | tf_op jit(solution)/shard_map/psum | solution.py:47
  133.8 0.7 slice_multiply_fusion.1
  134.4 13.0 %convolution_bitcast_fusion = f32[16,2048,64]{1,2,0:T(8,128)} fusion(bf16[16,256,2048]{2,1,0:T(8,128)(2,1)} %param.5, f32[16,256,64]{1,2,0:T(8,128)S(1)} %get-tuple-element.5, f32[16,256,64]{1,2,0:T(8,128)} %get-tuple-element.14, f32[16,64]{1,0:T(8,128)S(1)} %get-tuple-element.9), kind=kOutput, calls=%fused_computation.11 | convolution fusion | flops 1075056640 | bytes 27267072 | tf_op jit(solution)/shard_map/ltd,lte->lde/dot_general | solution.py:45
  147.4 0.0 all-reduce.3.cloned.1.call-update
  148.7 11.5 %convolution_convert_fusion = bf16[16,256,2048]{2,1,0:T(8,128)(2,1)} fusion(bf16[16,2048,64]{1,2,0:T(8,128)(2,1)} %param.9, f32[16,256,64]{1,2,0:T(8,128)S(1)} %get-tuple-element.5, f32[16,256,64]{1,2,0:T(8,128)} %get-tuple-element.14, f32[16,64]{1,0:T(8,128)S(1)} %get-tuple-element.9), kind=kOutput, calls=%fused_computation.6 | convolution fusion | flops 1083445248 | bytes 23072768 | tf_op jit(solution)/shard_map/lte,lde->ltd/dot_general | solution.py:44
  160.2 103.2 %all-reduce.3.cloned.1.call-done = f32[16,2048,64]{1,2,0:T(8,128)} async-done(((f32[16,2048,64]{1,2,0:T(8,128)}), f32[16,2048,64]{1,2,0:T(8,128)}) %all-reduce.3.cloned.1.call-update) | async-done | bytes 8388624 | tf_op jit(solution)/shard_map/psum | solution.py:46
  263.4 7.9 %copy.15 = f32[16,2048,64]{1,2,0:T(8,128)} copy(f32[16,2048,64]{1,2,0:T(8,128)} %all-reduce.3.cloned.1.call-done) | data formatting | bytes 16777216
  (1 shorter events, 0.0 us)
Async XLA Ops:
  7.2 12.1 %copy-start = (s32[16,256,8]{1,2,0:T(8,128)S(1)}, s32[16,256,8]{1,2,0:T(8,128)}, u32[]{:S(2)}) copy-start(s32[16,256,8]{1,2,0:T(8,128)} %param.6) | copy-start | bytes 393220
  7.2 256.2 %all-reduce.3.cloned.1.call-start = ((), (), s32[]{:S(2)}) async-start(), calls=%async_computation | async-start | bytes 16777216 | tf_op jit(solution)/shard_map/psum | solution.py:46
Sparse Core Ops, SparseCore 0:
  147.5 115.8 all-reduce.2
where the time goes:
time: 280 us; the launch traced here: 279 us
  matrix products  117 us (42%)
  waiting for transfers between devices  103 us (37%)
  blocking collectives  25.4 us (9%)
  between operations  16.5 us (6%)
  local copies, waits for them, and re-layouts  8.86 us (3%)
  other arithmetic  8.15 us (3%)
    psum x1, waiting for transfers between devices, local_step(): d_router = lax.psum(part_grad, 'dp')  103 us
    dot_general x1, matrix products, router_forward(): jnp.einsum('ltkd,ltd->ltk', expert_out, d_out, preferred_element_type=jnp...  82 us
    psum x1, blocking collectives, local_step(): total_loss = lax.psum(main_part, 'dp') + aux_total  25.4 us
    dot_general x1, matrix products, local_step(): jnp.einsum('ltd,lte->lde', u_norm, d_log16, preferred_element_type=jnp.fl...  13 us
    dot_general x1, matrix products, local_step(): jnp.einsum('lte,lde->ltd', d_log16, w_router, preferred_element_type=jnp....  11.5 us
    dot_general x1, matrix products, router_forward(): jnp.einsum('ltd,lde->lte', u_norm, w_router, preferred_element_type=jnp.f...  10.6 us
    unnamed x3, local copies, waits for them, and re-layouts  7.89 us
  transfers between devices with their start and end apart: 1, of which 1 were waited for; matrix products, arithmetic and copies ran while one was open for 4% of the time, Pallas kernels for 0%

commit v1 on v0

v1 whole, which is shorter than its diff:
```python
import jax
import jax.numpy as jnp
from jax import lax
from jax.experimental import pallas as pl
from jax.experimental.pallas import tpu as pltpu
from jax.sharding import PartitionSpec as P

AUX_COEF = 0.02
MESH = pl.DeviceIdType.MESH

NB = 8
NC = 4
NU = 3
AGL = 7

NT = (((1,), (1,)), ((), ()))
TN = (((0,), (0,)), ((), ()))


def step_kernel(n_lay, n_dev, tok_all, idx_hbm, eo_hbm, dy_hbm, u_hbm, w_hbm,
                fin, gout, wv, loss_out,
                idx_v, ebuf, ubuf, dbuf, part, rd, r1, r2, cnt_src, cnt_in, loss_src, loss_in,
                fcol, slot_v, loss_acc,
                idx_sem, e_sem, u_sem, d_sem, w_sem, cs_sem, cr_sem, ls_sem, lr_sem, s_sem, r_sem):
    me = lax.axis_index('dp')
    core = me % 2
    xpos = (me // 2) % 2
    ypos = me // 4
    partner = me + 1 - 2 * core
    xn = me + 2 - 4 * xpos
    yn = me + 4 - 8 * ypos
    nbr_a = xn * (1 - core) + yn * core
    nbr_b = yn * (1 - core) + xn * core
    pa = xpos * (1 - core) + ypos * core
    pb = ypos * (1 - core) + xpos * core
    half = 4 * core
    quart = half + 2 * pa
    mine = quart + pb
    n_exp = w_hbm.shape[1]
    top_k = idx_hbm.shape[1]
    tok = u_hbm.shape[1]
    rows = ebuf.shape[1]
    ctok = rows // top_k

    def e_copy(lay, c, slot):
        return pltpu.make_async_copy(eo_hbm.at[lay, pl.ds(c * rows, rows)], ebuf.at[slot], e_sem.at[slot])

    def u_copy(lay):
        return pltpu.make_async_copy(u_hbm.at[lay], ubuf.at[lay % NU], u_sem.at[lay % NU])

    def d_copy(lay):
        return pltpu.make_async_copy(dy_hbm.at[lay], dbuf.at[lay % NU], d_sem.at[lay % NU])

    def w_copy(lay):
        return pltpu.make_async_copy(w_hbm.at[lay], wv.at[lay], w_sem.at[lay])

    idx_copy = pltpu.make_async_copy(idx_hbm, idx_v, idx_sem)
    idx_copy.start()
    for c in range(2):
        if c == 0:
            w_copy(0).start()
            u_copy(0).start()
            d_copy(0).start()
        else:
            w_copy(1).start()
            u_copy(1).start()
            d_copy(1).start()
        for j in range(NC):
            e_copy(c, j, c * NC + j).start()

    barrier = pltpu.get_barrier_semaphore()
    for d in range(1, n_dev):
        pl.semaphore_signal(barrier, inc=1, device_id=((me + d) % n_dev,), device_id_type=MESH)

    idx_copy.wait()
    ones = jnp.ones((8, tok), jnp.bfloat16)
    row_id = lax.broadcasted_iota(jnp.int32, (8, 2 * n_exp), 0)
    e_id = lax.broadcasted_iota(jnp.int32, (n_exp, tok), 0)
    cnt = jnp.zeros((8, 2 * n_exp), jnp.float32)
    for r in range(n_lay // 2):
        hots = []
        for h in range(2):
            ids = idx_v[2 * r + h]
            acc = jnp.zeros((n_exp, tok), jnp.float32)
            for k in range(top_k):
                acc = jnp.where(e_id == ids[k:k + 1], 1.0, acc)
            hots.append(acc.astype(jnp.bfloat16))
        both = jnp.concatenate(hots, axis=0)
        res = lax.dot_general(ones, both, NT, preferred_element_type=jnp.float32)
        cnt = jnp.where(row_id == r, res, cnt)
    cnt_src[...] = cnt
    cnt_in[me] = cnt
    loss_acc[...] = jnp.zeros_like(loss_acc)
    pl.semaphore_wait(barrier, n_dev - 1)

    def cnt_copy(to, frm):
        return pltpu.make_async_remote_copy(
            src_ref=cnt_src, dst_ref=cnt_in.at[frm], send_sem=cs_sem.at[to], recv_sem=cr_sem.at[frm],
            device_id=(to,), device_id_type=MESH)

    def loss_copy(to, frm):
        return pltpu.make_async_remote_copy(
            src_ref=loss_src, dst_ref=loss_in.at[frm], send_sem=ls_sem.at[to], recv_sem=lr_sem.at[frm],
            device_id=(to,), device_id_type=MESH)

    for d in range(1, n_dev):
        cnt_copy((me + d) % n_dev, me).start()

    def rcopy(stage, src, dst, m, dev):
        return pltpu.make_async_remote_copy(
            src_ref=src, dst_ref=dst, send_sem=s_sem.at[stage, m], recv_sem=r_sem.at[stage, m],
            device_id=(dev,), device_id_type=MESH)

    def c_pair(m):
        return rcopy(0, part.at[m, pl.ds(4 - half, 4)], rd.at[m], m, partner)

    def c_rs1(m):
        return rcopy(1, part.at[m, pl.ds(half + 2 - 2 * pa, 2)], r1.at[m], m, nbr_a)

    def c_rs2(m):
        return rcopy(2, part.at[m, pl.ds(quart + 1 - pb, 1)], r2.at[m], m, nbr_b)

    def c_ag1(m, p):
        return rcopy(3, fin.at[m, pl.ds(p, 1)], fin.at[m, pl.ds(p, 1)], m, nbr_b)

    def c_ag2(m, p):
        return rcopy(4, fin.at[m, pl.ds(p, 2)], fin.at[m, pl.ds(p, 2)], m, nbr_a)

    def c_out(m, p):
        return rcopy(5, fin.at[m, pl.ds(p, 4)], fin.at[m, pl.ds(p, 4)], m, partner)

    def do_a(m):
        c_pair(m).wait_recv()
        o = 2 - 2 * pa
        part[m, pl.ds(half + o, 2)] += rd[m, pl.ds(o, 2)]
        part[m, pl.ds(quart, 2)] += rd[m, pl.ds(2 * pa, 2)]
        c_rs1(m).start()

    def do_b(m):
        c_rs1(m).wait_recv()
        o = 1 - pb
        part[m, pl.ds(quart + o, 1)] += r1[m, pl.ds(o, 1)]
        part[m, pl.ds(mine, 1)] += r1[m, pl.ds(pb, 1)]
        c_rs2(m).start()

    def do_c(m):
        c_rs2(m).wait_recv()
        fin[m, pl.ds(mine, 1)] = part[m, pl.ds(mine, 1)] + r2[m]

    def do_ag1(m):
        c_ag1(m, mine).start()

    def do_d(m):
        c_ag1(m, quart + 1 - pb).wait_recv()
        c_ag2(m, quart).start()

    def do_e(m):
        c_ag2(m, half + 2 - 2 * pa).wait_recv()
        c_out(m, half).start()

    def do_f(m):
        c_out(m, 4 - half).wait_recv()

    def slot_chunk(lay, c, slot):
        e_copy(lay, c, slot).wait()
        lanes = 2 * ctok
        lo = (c // 2) * lanes
        dcols = dbuf[lay % NU, lo:lo + lanes, :]
        s = lax.dot_general(ebuf[slot], dcols, NT, preferred_element_type=jnp.float32)
        lane = lax.broadcasted_iota(jnp.int32, (top_k, lanes), 1)
        acc = jnp.zeros((top_k, lanes), jnp.float32)
        for i in range(ctok):
            acc = jnp.where(lane == (c % 2) * ctok + i, s[i * top_k:(i + 1) * top_k], acc)
        if c % 2:
            slot_v[:, lo:lo + lanes] += acc
        else:
            slot_v[:, lo:lo + lanes] = acc

        @pl.when(lay + 2 < n_lay)
        def _():
            e_copy(lay + 2, c, slot).start()

    scale = float(tok_all)
    pull = AUX_COEF * n_exp / (top_k * tok_all)

    @pl.loop(0, n_lay)
    def _(lay):
        @pl.when(lay + 2 < n_lay)
        def _():
            w_copy(lay + 2).start()
            u_copy(lay + 2).start()
            d_copy(lay + 2).start()

        base = (lay % 2) * NC
        w_copy(lay).wait()
        u_copy(lay).wait()
        d_copy(lay).wait()
        slot_chunk(lay, 0, base)

        @pl.when(lay >= 1)
        def _():
            do_a(lay - 1)

        slot_chunk(lay, 1, base + 1)

        @pl.when(lay >= 2)
        def _():
            do_b(lay - 2)

        slot_chunk(lay, 2, base + 2)

        @pl.when(lay >= 3)
        def _():
            do_c(lay - 3)

            @pl.when(lay - 3 < AGL)
            def _():
                do_ag1(lay - 3)

        slot_chunk(lay, 3, base + 3)

        @pl.when(jnp.logical_and(lay >= 4, lay - 4 < AGL))
        def _():
            do_d(lay - 4)

        @pl.when(jnp.logical_and(lay >= 5, lay - 5 < AGL))
        def _():
            do_e(lay - 5)

        u = ubuf[lay % NU]
        logits = lax.dot_general(wv[lay], u, NT, preferred_element_type=jnp.float32)
        ex = jnp.exp(logits - jnp.max(logits, axis=0, keepdims=True))
        prob = ex / jnp.sum(ex, axis=0, keepdims=True)
        ids = idx_v[lay]
        chosen = jnp.concatenate(
            [jnp.sum(jnp.where(e_id == ids[k:k + 1], logits, 0.0), axis=0, keepdims=True) for k in range(top_k)], axis=0)
        ge = jnp.exp(chosen - jnp.max(chosen, axis=0, keepdims=True))
        gate = ge / jnp.sum(ge, axis=0, keepdims=True)

        @pl.when(lay == 0)
        def _():
            for d in range(1, n_dev):
                cnt_copy((me + d) % n_dev, (me + d) % n_dev).wait_recv()
            tot = cnt_in[0]
            for j in range(1, n_dev):
                tot = tot + cnt_in[j]
            cols = jnp.transpose(tot * pull)
            for i in range(n_lay):
                o = (i % 2) * n_exp
                fcol[i] = jnp.broadcast_to(cols[o:o + n_exp, i // 2:i // 2 + 1], (n_exp, fcol.shape[2]))

        slots = slot_v[...]
        dd = scale * slots
        dch = gate * (dd - jnp.sum(gate * dd, axis=0, keepdims=True))
        fc = fcol[lay]
        fa = jnp.concatenate([fc] * (tok // fc.shape[1]), axis=1)
        pf = prob * fa
        pf_sum = jnp.sum(pf, axis=0, keepdims=True)
        g = pf - prob * pf_sum
        for k in range(top_k):
            g = g + jnp.where(e_id == ids[k:k + 1], dch[k:k + 1], 0.0)
        main = gate * slots
        first = lax.broadcasted_iota(jnp.int32, (top_k, tok), 0) == 0
        main = main + jnp.where(first, pf_sum * (1.0 / tok_all), 0.0)
        loss_acc[...] += main
        g16 = g.astype(jnp.bfloat16)
        gout[lay] = g16
        pg = jnp.dot(g16, u, preferred_element_type=jnp.float32)
        part[lay] = pg.reshape(part.shape[1:])
        c_pair(lay).start()

    last = n_lay - 1
    la = loss_acc[...]
    lv = la[:, :128]
    for j in range(1, tok // 128):
        lv = lv + la[:, 128 * j:128 * (j + 1)]
    loss_src[...] = lv
    loss_in[me] = lv
    do_a(last)
    do_b(last - 1)
    for d in range(1, n_dev):
        loss_copy((me + d) % n_dev, me).start()
    do_c(last - 2)

    @pl.loop(AGL, last - 1)
    def _(m):
        do_ag1(m)

    do_b(last)
    do_c(last - 1)
    do_ag1(last - 1)

    @pl.loop(AGL, last - 1)
    def _(m):
        do_d(m)

    do_c(last)
    do_ag1(last)
    do_d(last - 1)

    @pl.loop(AGL, last - 1)
    def _(m):
        do_e(m)

    do_d(last)
    do_e(last - 1)
    do_e(last)

    for d in range(1, n_dev):
        loss_copy((me + d) % n_dev, (me + d) % n_dev).wait_recv()
    tot = loss_in[0]
    for j in range(1, n_dev):
        tot = tot + loss_in[j]
    loss_out[...] = tot
    for d in range(1, n_dev):
        cnt_copy((me + d) % n_dev, me).wait_send()
        loss_copy((me + d) % n_dev, me).wait_send()

    @pl.loop(0, n_lay)
    def _(m):
        do_f(m)
        c_pair(m).wait_send()
        c_rs1(m).wait_send()
        c_rs2(m).wait_send()
        c_ag1(m, mine).wait_send()
        c_ag2(m, quart).wait_send()
        c_out(m, half).wait_send()


NS = 4


def out_kernel(n_lay, g_v, w_v, f_v, l_v, dn_hbm, dr_hbm, loss, stage, st_sem, f_sem):
    f_copy = pltpu.make_async_copy(f_v, dr_hbm, f_sem)

    def put(lay):
        return pltpu.make_async_copy(stage.at[lay % NS], dn_hbm.at[lay], st_sem.at[lay % NS])

    f_copy.start()
    loss[0, 0] = jnp.sum(l_v[...])

    @pl.loop(0, n_lay)
    def _(lay):
        @pl.when(lay >= NS)
        def _():
            put(lay - NS).wait()

        dn = lax.dot_general(g_v[lay], w_v[lay], TN, preferred_element_type=jnp.float32)
        stage[lay % NS] = dn.astype(jnp.bfloat16)
        put(lay).start()

    for i in range(NS):
        put(n_lay - NS + i).wait()
    f_copy.wait()


def solution(mesh):
    n_dev = mesh.shape['dp']

    def local_step(u_norm, expert_idx, expert_out, d_out, w_router):
        n_lay, tok, dim = u_norm.shape
        n_exp = w_router.shape[2]
        top_k = expert_idx.shape[2]
        tok_all = tok * n_dev
        f32, bf16 = jnp.float32, jnp.bfloat16
        idx_t = jnp.swapaxes(expert_idx, 1, 2)
        w_t = jnp.swapaxes(w_router, 1, 2)
        eo = expert_out.reshape(n_lay, tok * top_k, dim)
        rows = tok * top_k // NC
        pieces = 8
        prow = n_exp // pieces
        any_spec = pl.BlockSpec(memory_space=pl.ANY)
        vm_spec = pl.BlockSpec(memory_space=pltpu.VMEM)
        dma = pltpu.SemaphoreType.DMA
        fin, g_all, w_all, loss_v = pl.pallas_call(
            lambda *refs: step_kernel(n_lay, n_dev, tok_all, *refs),
            out_shape=(
                pltpu.VMEM((n_lay, pieces, prow, dim), f32),
                pltpu.VMEM((n_lay, n_exp, tok), bf16),
                pltpu.VMEM((n_lay, n_exp, dim), bf16),
                pltpu.VMEM((8, 128), f32),
            ),
            in_specs=[any_spec] * 5,
            out_specs=(vm_spec,) * 4,
            scratch_shapes=[
                pltpu.VMEM((n_lay, top_k, tok), jnp.int32),
                pltpu.VMEM((NB, rows, dim), bf16),
                pltpu.VMEM((NU, tok, dim), bf16),
                pltpu.VMEM((NU, tok, dim), bf16),
                pltpu.VMEM((n_lay, pieces, prow, dim), f32),
                pltpu.VMEM((n_lay, pieces // 2, prow, dim), f32),
                pltpu.VMEM((n_lay, pieces // 4, prow, dim), f32),
                pltpu.VMEM((n_lay, pieces // 8, prow, dim), f32),
                pltpu.VMEM((8, 128), f32),
                pltpu.VMEM((n_dev, 8, 128), f32),
                pltpu.VMEM((8, 128), f32),
                pltpu.VMEM((n_dev, 8, 128), f32),
                pltpu.VMEM((n_lay, n_exp, 128), f32),
                pltpu.VMEM((top_k, tok), f32),
                pltpu.VMEM((top_k, tok), f32),
                dma, dma((NB,)), dma((NU,)), dma((NU,)), dma((n_lay,)),
                dma((n_dev,)), dma((n_dev,)), dma((n_dev,)), dma((n_dev,)),
                dma((6, n_lay)), dma((6, n_lay)),
            ],
            compiler_params=pltpu.CompilerParams(
                collective_id=0, has_side_effects=True, vmem_limit_bytes=48 << 20),
            name='router_step',
        )(idx_t, eo, d_out, u_norm, w_t)
        d_norm, d_rt, loss = pl.pallas_call(
            lambda *refs: out_kernel(n_lay, *refs),
            out_shape=(
                jax.ShapeDtypeStruct((n_lay, tok, dim), bf16),
                jax.ShapeDtypeStruct((n_lay, pieces, prow, dim), f32),
                jax.ShapeDtypeStruct((1, 1), f32),
            ),
            in_specs=[vm_spec] * 4,
            out_specs=(any_spec, any_spec, pl.BlockSpec(memory_space=pltpu.SMEM)),
            scratch_shapes=[pltpu.VMEM((NS, tok, dim), bf16), dma((NS,)), dma],
            compiler_params=pltpu.CompilerParams(vmem_limit_bytes=12 << 20),
            name='router_out',
        )(g_all, w_all, fin, loss_v)
        d_router = jnp.swapaxes(d_rt.reshape(n_lay, n_exp, dim), 1, 2)
        return loss[0, 0], d_router, d_norm

    tok_spec = P(None, 'dp', None)
    return jax.shard_map(local_step, mesh=mesh, in_specs=(tok_spec, tok_spec, P(None, 'dp', None, None), tok_spec, P()), out_specs=(P(), P(), tok_spec), check_vma=False)
```

time: 280 us -> 149 us (0.53)
  Pallas kernels: 0 us -> 149 us
  matrix products: 117 us -> 0 us
  waiting for transfers between devices: 103 us -> 0 us
  blocking collectives: 25.4 us -> 0 us
  between operations: 16.5 us -> 0.64 us
  local copies, waits for them, and re-layouts: 8.86 us -> 0 us
  other arithmetic: 8.15 us -> 0 us
    pallas_call x0 -> x2, Pallas kernels: none -> 149 us  [the longest x1 138 us: local_step(): pl.pallas_call(lambda *refs: step_kernel(n_lay, n_dev, tok_all, *refs), o...]
    dot_general x4 -> x0, matrix products: 117 us -> none  [the longest x1 82 us: router_forward(): jnp.einsum('ltkd,ltd->ltk', expert_out, d_out, preferred_element_type=jnp...]
    psum x1 -> x0, waiting for transfers between devices: 103 us -> none  [local_step(): d_router = lax.psum(part_grad, 'dp')]
    psum x1 -> x0, blocking collectives: 25.4 us -> none  [local_step(): total_loss = lax.psum(main_part, 'dp') + aux_total]
    unnamed x3 -> x0, local copies, waits for them, and re-layouts: 7.89 us -> none
    reduce_sum x3 -> x0, other arithmetic: 4.98 us -> none  [the longest x1 2.62 us: router_forward(): chosen = jnp.sum(one_hot * logits[:, :, None, :], axis=-1)]
  transfers between devices with their start and end apart: 1 -> 0, of which waited for: 1 -> 0; matrix products, arithmetic and copies ran while one was open for 4% -> 0% of each run, Pallas kernels for 0% -> 0%
where the time goes in v1:
time: 149 us
  Pallas kernels  149 us (100%)
    pallas_call x1, Pallas kernels, local_step(): pl.pallas_call(lambda *refs: step_kernel(n_lay, n_dev, tok_all, *refs), o...  138 us
    pallas_call x1, Pallas kernels, local_step(): pl.pallas_call(lambda *refs: out_kernel(n_lay, *refs), out_shape=(jax.Sha...  10.7 us

profile of v1, /device:TPU:0, one launch (start us, length us, event | category | flops | bytes accessed | tf_op | source)
XLA Modules:
  0.0 149.3 jit_solution(7406222740381940363)
XLA Ops:
  0.6 138.0 %router_step.1 = (f32[16,8,8,2048]{3,2,1,0:T(8,128)S(1)}, bf16[16,64,256]{2,1,0:T(8,128)(2,1)S(1)}, bf16[16,64,2048]{2,1,0:T(8,128)(2,1)S(1)}, f32[8,128]{1,0:T(8,128)S(1)}) custom-call(s32[16,8,256]{2,1,0:T(8,128)} %bitcast.8, bf16[16,2048,2048]{2,1,0:T(8,128)(2,1)} %bitcast.1.refs_1_, bf16[16,256,2048]{2,1,0:T(8,128)(2,1)} %refs_2_.1, ...), custom_call_target="tpu_custom_call" | custom-call | tf_op jit(solution)/shard_map/router_step/pallas_call | solution.py:375
  138.6 10.7 %router_out.1 = (bf16[16,256,2048]{2,1,0:T(8,128)(2,1)}, f32[16,8,8,2048]{3,2,1,0:T(8,128)}, f32[1,1]{1,0:T(1,128)}) custom-call(bf16[16,64,256]{2,1,0:T(8,128)(2,1)S(1)} %get-tuple-element.10.refs_0_, bf16[16,64,2048]{2,1,0:T(8,128)(2,1)S(1)} %get-tuple-element.11.refs_1_, f32[16,8,8,2048]{3,2,1,0:T(8,128)S(1)} %get-tuple-element.12.refs_2_, ...), custom_call_target="tpu_custom_call" | custom-call | tf_op jit(solution)/shard_map/router_out/pallas_call | solution.py:409

commit v2 on v1

--- a/solution.py
+++ b/solution.py
@@ -166,11 +166,13 @@
         lanes = 2 * ctok
         lo = (c // 2) * lanes
         dcols = dbuf[lay % NU, lo:lo + lanes, :]
-        s = lax.dot_general(ebuf[slot], dcols, NT, preferred_element_type=jnp.float32)
+        hr = rows // 2
+        s = [lax.dot_general(ebuf[slot, h * hr:(h + 1) * hr, :], dcols, NT, preferred_element_type=jnp.float32) for h in range(2)]
         lane = lax.broadcasted_iota(jnp.int32, (top_k, lanes), 1)
         acc = jnp.zeros((top_k, lanes), jnp.float32)
         for i in range(ctok):
-            acc = jnp.where(lane == (c % 2) * ctok + i, s[i * top_k:(i + 1) * top_k], acc)
+            j = i * top_k
+            acc = jnp.where(lane == (c % 2) * ctok + i, s[j // hr][j % hr:j % hr + top_k], acc)
         if c % 2:
             slot_v[:, lo:lo + lanes] += acc
         else:

time: 149 us -> 125 us (0.84)
  Pallas kernels: 149 us -> 125 us
    pallas_call x1, Pallas kernels: 138 us -> 114 us  [local_step(): pl.pallas_call(lambda *refs: step_kernel(n_lay, n_dev, tok_all, *refs), o...]
where the time goes in v2:
time: 125 us
  Pallas kernels  125 us (100%)
    pallas_call x1, Pallas kernels, local_step(): pl.pallas_call(lambda *refs: step_kernel(n_lay, n_dev, tok_all, *refs), o...  114 us
    pallas_call x1, Pallas kernels, local_step(): pl.pallas_call(lambda *refs: out_kernel(n_lay, *refs), out_shape=(jax.Sha...  10.7 us

profile of v2, /device:TPU:0, one launch (start us, length us, event | category | flops | bytes accessed | tf_op | source)
XLA Modules:
  0.0 125.3 jit_solution(16767969801952095111)
XLA Ops:
  0.6 114.0 %router_step.1 = (f32[16,8,8,2048]{3,2,1,0:T(8,128)S(1)}, bf16[16,64,256]{2,1,0:T(8,128)(2,1)S(1)}, bf16[16,64,2048]{2,1,0:T(8,128)(2,1)S(1)}, f32[8,128]{1,0:T(8,128)S(1)}) custom-call(s32[16,8,256]{2,1,0:T(8,128)} %bitcast.8, bf16[16,2048,2048]{2,1,0:T(8,128)(2,1)} %bitcast.1.refs_1_, bf16[16,256,2048]{2,1,0:T(8,128)(2,1)} %refs_2_.1, ...), custom_call_target="tpu_custom_call" | custom-call | tf_op jit(solution)/shard_map/router_step/pallas_call | solution.py:377
  114.6 10.7 %router_out.1 = (bf16[16,256,2048]{2,1,0:T(8,128)(2,1)}, f32[16,8,8,2048]{3,2,1,0:T(8,128)}, f32[1,1]{1,0:T(1,128)}) custom-call(bf16[16,64,256]{2,1,0:T(8,128)(2,1)S(1)} %get-tuple-element.10.refs_0_, bf16[16,64,2048]{2,1,0:T(8,128)(2,1)S(1)} %get-tuple-element.11.refs_1_, f32[16,8,8,2048]{3,2,1,0:T(8,128)S(1)} %get-tuple-element.12.refs_2_, ...), custom_call_target="tpu_custom_call" | custom-call | tf_op jit(solution)/shard_map/router_out/pallas_call | solution.py:411

commit v3 on v2

--- a/solution.py
+++ b/solution.py
@@ -11,7 +11,6 @@
 NB = 8
 NC = 4
 NU = 3
-AGL = 7
 
 NT = (((1,), (1,)), ((), ()))
 TN = (((0,), (0,)), ((), ()))
@@ -20,7 +19,7 @@
 def step_kernel(n_lay, n_dev, tok_all, idx_hbm, eo_hbm, dy_hbm, u_hbm, w_hbm,
                 fin, gout, wv, loss_out,
                 idx_v, ebuf, ubuf, dbuf, part, rd, r1, r2, cnt_src, cnt_in, loss_src, loss_in,
-                fcol, slot_v, loss_acc,
+                fcol, slot_v, lg_v, loss_acc,
                 idx_sem, e_sem, u_sem, d_sem, w_sem, cs_sem, cr_sem, ls_sem, lr_sem, s_sem, r_sem):
     me = lax.axis_index('dp')
     core = me % 2
@@ -161,83 +160,131 @@
     def do_f(m):
         c_out(m, 4 - half).wait_recv()
 
+    hr = rows // 2
+    lanes = 2 * ctok
+    lane = lax.broadcasted_iota(jnp.int32, (top_k, lanes), 1)
+    e_half = lax.broadcasted_iota(jnp.int32, (n_exp, lanes), 0)
+    first = lax.broadcasted_iota(jnp.int32, (top_k, lanes), 0) == 0
+    scale = float(tok_all)
+    pull = AUX_COEF * n_exp / (top_k * tok_all)
+
     def slot_chunk(lay, c, slot):
-        e_copy(lay, c, slot).wait()
-        lanes = 2 * ctok
         lo = (c // 2) * lanes
         dcols = dbuf[lay % NU, lo:lo + lanes, :]
-        hr = rows // 2
         s = [lax.dot_general(ebuf[slot, h * hr:(h + 1) * hr, :], dcols, NT, preferred_element_type=jnp.float32) for h in range(2)]
-        lane = lax.broadcasted_iota(jnp.int32, (top_k, lanes), 1)
         acc = jnp.zeros((top_k, lanes), jnp.float32)
         for i in range(ctok):
             j = i * top_k
             acc = jnp.where(lane == (c % 2) * ctok + i, s[j // hr][j % hr:j % hr + top_k], acc)
         if c % 2:
-            slot_v[:, lo:lo + lanes] += acc
+            slot_v[lay % 2, :, lo:lo + lanes] += acc
         else:
-            slot_v[:, lo:lo + lanes] = acc
-
-        @pl.when(lay + 2 < n_lay)
-        def _():
-            e_copy(lay + 2, c, slot).start()
-
-    scale = float(tok_all)
-    pull = AUX_COEF * n_exp / (top_k * tok_all)
+            slot_v[lay % 2, :, lo:lo + lanes] = acc
+
+    def logit_part(lay):
+        for h in range(2):
+            lo = h * lanes
+            lg_v[:, lo:lo + lanes] = lax.dot_general(
+                wv[lay], ubuf[lay % NU, lo:lo + lanes, :], NT, preferred_element_type=jnp.float32)
+
+    def g_part(lay, h, keep):
+        lo = h * lanes
+        logits = lg_v[:, lo:lo + lanes]
+        ids = idx_v[lay, :, lo:lo + lanes]
+        ex = jnp.exp(logits - jnp.max(logits, axis=0, keepdims=True))
+        prob = ex / jnp.sum(ex, axis=0, keepdims=True)
+        chosen = jnp.concatenate(
+            [jnp.sum(jnp.where(e_half == ids[k:k + 1], logits, 0.0), axis=0, keepdims=True) for k in range(top_k)], axis=0)
+        ge = jnp.exp(chosen - jnp.max(chosen, axis=0, keepdims=True))
+        gate = ge / jnp.sum(ge, axis=0, keepdims=True)
+        slots = slot_v[lay % 2, :, lo:lo + lanes]
+        dd = scale * slots
+        dch = gate * (dd - jnp.sum(gate * dd, axis=0, keepdims=True))
+        pf = prob * fcol[lay]
+        pf_sum = jnp.sum(pf, axis=0, keepdims=True)
+        g = pf - prob * pf_sum
+        for k in range(top_k):
+            g = g + jnp.where(e_half == ids[k:k + 1], dch[k:k + 1], 0.0)
+        main = gate * slots + jnp.where(first, pf_sum * (1.0 / tok_all), 0.0)
+        total = loss_acc[:, lo:lo + lanes] + main
+        loss_acc[:, lo:lo + lanes] = total if keep is None else jnp.where(keep, total, 0.0)
+        gout[lay, :, lo:lo + lanes] = g.astype(jnp.bfloat16)
+
+    def p_part(lay):
+        dim = ubuf.shape[2]
+        for h in range(2):
+            lo = h * (dim // 2)
+            pg = jnp.dot(gout[lay], ubuf[lay % NU, :, lo:lo + dim // 2], preferred_element_type=jnp.float32)
+            part[lay, :, :, lo:lo + dim // 2] = pg.reshape(part.shape[1:3] + (dim // 2,))
+
+    slot_v[...] = jnp.zeros_like(slot_v)
+    lg_v[...] = jnp.zeros_like(lg_v)
+    fcol[0] = jnp.zeros(fcol.shape[1:], jnp.float32)
 
     @pl.loop(0, n_lay)
     def _(lay):
+        base = (lay % 2) * NC
+        prev = jnp.maximum(lay - 1, 0)
+        keep = lay >= 1
+
+        def refill(c):
+            @pl.when(lay + 2 < n_lay)
+            def _():
+                e_copy(lay + 2, c, base + c).start()
+
+        @pl.when(lay >= 2)
+        def _():
+            do_a(lay - 2)
+
+        w_copy(lay).wait()
+        u_copy(lay).wait()
+        d_copy(lay).wait()
+        e_copy(lay, 0, base).wait()
+        slot_chunk(lay, 0, base)
+        g_part(prev, 0, keep)
+        refill(0)
+
+        @pl.when(lay >= 3)
+        def _():
+            do_b(lay - 3)
+
+        e_copy(lay, 1, base + 1).wait()
+        slot_chunk(lay, 1, base + 1)
+        g_part(prev, 1, keep)
+        refill(1)
+
+        @pl.when(lay >= 4)
+        def _():
+            do_c(lay - 4)
+            do_ag1(lay - 4)
+
+        e_copy(lay, 2, base + 2).wait()
+        slot_chunk(lay, 2, base + 2)
+        p_part(prev)
+        refill(2)
+
         @pl.when(lay + 2 < n_lay)
         def _():
             w_copy(lay + 2).start()
             u_copy(lay + 2).start()
             d_copy(lay + 2).start()
 
-        base = (lay % 2) * NC
-        w_copy(lay).wait()
-        u_copy(lay).wait()
-        d_copy(lay).wait()
-        slot_chunk(lay, 0, base)
-
         @pl.when(lay >= 1)
         def _():
-            do_a(lay - 1)
-
-        slot_chunk(lay, 1, base + 1)
-
-        @pl.when(lay >= 2)
-        def _():
-            do_b(lay - 2)
-
-        slot_chunk(lay, 2, base + 2)
-
-        @pl.when(lay >= 3)
-        def _():
-            do_c(lay - 3)
-
-            @pl.when(lay - 3 < AGL)
-            def _():
-                do_ag1(lay - 3)
-
+            c_pair(lay - 1).start()
+
+        @pl.when(lay >= 5)
+        def _():
+            do_d(lay - 5)
+
+        e_copy(lay, 3, base + 3).wait()
         slot_chunk(lay, 3, base + 3)
-
-        @pl.when(jnp.logical_and(lay >= 4, lay - 4 < AGL))
-        def _():
-            do_d(lay - 4)
-
-        @pl.when(jnp.logical_and(lay >= 5, lay - 5 < AGL))
-        def _():
-            do_e(lay - 5)
-
-        u = ubuf[lay % NU]
-        logits = lax.dot_general(wv[lay], u, NT, preferred_element_type=jnp.float32)
-        ex = jnp.exp(logits - jnp.max(logits, axis=0, keepdims=True))
-        prob = ex / jnp.sum(ex, axis=0, keepdims=True)
-        ids = idx_v[lay]
-        chosen = jnp.concatenate(
-            [jnp.sum(jnp.where(e_id == ids[k:k + 1], logits, 0.0), axis=0, keepdims=True) for k in range(top_k)], axis=0)
-        ge = jnp.exp(chosen - jnp.max(chosen, axis=0, keepdims=True))
-        gate = ge / jnp.sum(ge, axis=0, keepdims=True)
+        logit_part(lay)
+        refill(3)
+
+        @pl.when(lay >= 6)
+        def _():
+            do_e(lay - 6)
 
         @pl.when(lay == 0)
         def _():
@@ -251,62 +298,31 @@
                 o = (i % 2) * n_exp
                 fcol[i] = jnp.broadcast_to(cols[o:o + n_exp, i // 2:i // 2 + 1], (n_exp, fcol.shape[2]))
 
-        slots = slot_v[...]
-        dd = scale * slots
-        dch = gate * (dd - jnp.sum(gate * dd, axis=0, keepdims=True))
-        fc = fcol[lay]
-        fa = jnp.concatenate([fc] * (tok // fc.shape[1]), axis=1)
-        pf = prob * fa
-        pf_sum = jnp.sum(pf, axis=0, keepdims=True)
-        g = pf - prob * pf_sum
-        for k in range(top_k):
-            g = g + jnp.where(e_id == ids[k:k + 1], dch[k:k + 1], 0.0)
-        main = gate * slots
-        first = lax.broadcasted_iota(jnp.int32, (top_k, tok), 0) == 0
-        main = main + jnp.where(first, pf_sum * (1.0 / tok_all), 0.0)
-        loss_acc[...] += main
-        g16 = g.astype(jnp.bfloat16)
-        gout[lay] = g16
-        pg = jnp.dot(g16, u, preferred_element_type=jnp.float32)
-        part[lay] = pg.reshape(part.shape[1:])
-        c_pair(lay).start()
-
     last = n_lay - 1
+    for h in range(2):
+        g_part(last, h, None)
+    p_part(last)
     la = loss_acc[...]
     lv = la[:, :128]
     for j in range(1, tok // 128):
         lv = lv + la[:, 128 * j:128 * (j + 1)]
     loss_src[...] = lv
     loss_in[me] = lv
-    do_a(last)
-    do_b(last - 1)
-    for d in range(1, n_dev):
-        loss_copy((me + d) % n_dev, me).start()
-    do_c(last - 2)
-
-    @pl.loop(AGL, last - 1)
-    def _(m):
+    c_pair(last).start()
+
+    def do_cg(m):
+        do_c(m)
         do_ag1(m)
 
-    do_b(last)
-    do_c(last - 1)
-    do_ag1(last - 1)
-
-    @pl.loop(AGL, last - 1)
-    def _(m):
-        do_d(m)
-
-    do_c(last)
-    do_ag1(last)
-    do_d(last - 1)
-
-    @pl.loop(AGL, last - 1)
-    def _(m):
-        do_e(m)
-
-    do_d(last)
-    do_e(last - 1)
-    do_e(last)
+    steps = (do_a, do_b, do_cg, do_d, do_e)
+    for r in range(6):
+        for j in range(5):
+            m = last - 1 + r - j
+            if m <= last and j >= r - 1:
+                steps[j](m)
+        if r == 0:
+            for d in range(1, n_dev):
+                loss_copy((me + d) % n_dev, me).start()
 
     for d in range(1, n_dev):
         loss_copy((me + d) % n_dev, (me + d) % n_dev).wait_recv()
@@ -329,31 +345,26 @@
         c_out(m, half).wait_send()
 
 
-NS = 4
-
-
 def out_kernel(n_lay, g_v, w_v, f_v, l_v, dn_hbm, dr_hbm, loss, stage, st_sem, f_sem):
-    f_copy = pltpu.make_async_copy(f_v, dr_hbm, f_sem)
-
     def put(lay):
-        return pltpu.make_async_copy(stage.at[lay % NS], dn_hbm.at[lay], st_sem.at[lay % NS])
-
-    f_copy.start()
-    loss[0, 0] = jnp.sum(l_v[...])
+        return pltpu.make_async_copy(stage.at[lay], dn_hbm.at[lay], st_sem.at[lay])
+
+    def put_f(lay):
+        return pltpu.make_async_copy(f_v.at[lay], dr_hbm.at[lay], f_sem.at[lay])
 
     @pl.loop(0, n_lay)
     def _(lay):
-        @pl.when(lay >= NS)
-        def _():
-            put(lay - NS).wait()
-
+        put_f(lay).start()
         dn = lax.dot_general(g_v[lay], w_v[lay], TN, preferred_element_type=jnp.float32)
-        stage[lay % NS] = dn.astype(jnp.bfloat16)
+        stage[lay] = dn.astype(jnp.bfloat16)
         put(lay).start()
 
-    for i in range(NS):
-        put(n_lay - NS + i).wait()
-    f_copy.wait()
+    loss[0, 0] = jnp.sum(l_v[...])
+
+    @pl.loop(0, n_lay)
+    def _(lay):
+        put(lay).wait()
+        put_f(lay).wait()
 
 
 def solution(mesh):
@@ -398,7 +409,8 @@
                 pltpu.VMEM((8, 128), f32),
                 pltpu.VMEM((n_dev, 8, 128), f32),
                 pltpu.VMEM((n_lay, n_exp, 128), f32),
-                pltpu.VMEM((top_k, tok), f32),
+                pltpu.VMEM((2, top_k, tok), f32),
+                pltpu.VMEM((n_exp, tok), f32),
                 pltpu.VMEM((top_k, tok), f32),
                 dma, dma((NB,)), dma((NU,)), dma((NU,)), dma((n_lay,)),
                 dma((n_dev,)), dma((n_dev,)), dma((n_dev,)), dma((n_dev,)),
@@ -417,8 +429,8 @@
             ),
             in_specs=[vm_spec] * 4,
             out_specs=(any_spec, any_spec, pl.BlockSpec(memory_space=pltpu.SMEM)),
-            scratch_shapes=[pltpu.VMEM((NS, tok, dim), bf16), dma((NS,)), dma],
-            compiler_params=pltpu.CompilerParams(vmem_limit_bytes=12 << 20),
+            scratch_shapes=[pltpu.VMEM((n_lay, tok, dim), bf16), dma((n_lay,)), dma((n_lay,))],
+            compiler_params=pltpu.CompilerParams(vmem_limit_bytes=20 << 20),
             name='router_out',
         )(g_all, w_all, fin, loss_v)
         d_router = jnp.swapaxes(d_rt.reshape(n_lay, n_exp, dim), 1, 2)

time: 125 us -> 109 us (0.87)
  Pallas kernels: 125 us -> 108 us
    pallas_call x1, Pallas kernels: 114 us -> 98.4 us  [local_step(): pl.pallas_call(lambda *refs: step_kernel(n_lay, n_dev, tok_all, *refs), o...]
    pallas_call x1, Pallas kernels: 10.7 us -> 9.43 us  [local_step(): pl.pallas_call(lambda *refs: out_kernel(n_lay, *refs), out_shape=(jax.Sha...]
where the time goes in v3:
time: 109 us
  Pallas kernels  108 us (99%)
    pallas_call x1, Pallas kernels, local_step(): pl.pallas_call(lambda *refs: step_kernel(n_lay, n_dev, tok_all, *refs), o...  98.4 us
    pallas_call x1, Pallas kernels, local_step(): pl.pallas_call(lambda *refs: out_kernel(n_lay, *refs), out_shape=(jax.Sha...  9.43 us

profile of v3, /device:TPU:0, one launch (start us, length us, event | category | flops | bytes accessed | tf_op | source)
XLA Modules:
  0.0 108.5 jit_solution(11764702613597280331)
XLA Ops:
  0.6 98.4 %router_step.1 = (f32[16,8,8,2048]{3,2,1,0:T(8,128)S(1)}, bf16[16,64,256]{2,1,0:T(8,128)(2,1)S(1)}, bf16[16,64,2048]{2,1,0:T(8,128)(2,1)S(1)}, f32[8,128]{1,0:T(8,128)S(1)}) custom-call(s32[16,8,256]{2,1,0:T(8,128)} %bitcast.8, bf16[16,2048,2048]{2,1,0:T(8,128)(2,1)} %bitcast.1.refs_1_, bf16[16,256,2048]{2,1,0:T(8,128)(2,1)} %refs_2_.1, ...), custom_call_target="tpu_custom_call" | custom-call | tf_op jit(solution)/shard_map/router_step/pallas_call | solution.py:388
  99.1 9.4 %router_out.1 = (bf16[16,256,2048]{2,1,0:T(8,128)(2,1)}, f32[16,8,8,2048]{3,2,1,0:T(8,128)}, f32[1,1]{1,0:T(1,128)}) custom-call(bf16[16,64,256]{2,1,0:T(8,128)(2,1)S(1)} %get-tuple-element.10.refs_0_, bf16[16,64,2048]{2,1,0:T(8,128)(2,1)S(1)} %get-tuple-element.11.refs_1_, f32[16,8,8,2048]{3,2,1,0:T(8,128)S(1)} %get-tuple-element.12.refs_2_, ...), custom_call_target="tpu_custom_call" | custom-call | tf_op jit(solution)/shard_map/router_out/pallas_call | solution.py:423

commit v4 on v3

--- a/solution.py
+++ b/solution.py
@@ -11,6 +11,12 @@
 NB = 8
 NC = 4
 NU = 3
+AGL = 10
+LAG = {'a': (2, 1), 'b': (3, 3), 'c': (4, 3), 'g': (4, 3), 'd': (6, 0), 'e': (7, 3)}
+FIRST = {'a': (1, 2), 'b': (2, 3), 'c': (3, 3), 'g': (3, 3), 'd': (4, 3), 'e': (6, 1)}
+DRAIN = (('a', 1), ('g', 5), ('e', 6), ('g', 4), ('a', 0), ('b', 2), ('c', 3), ('g', 3), ('d', 5), ('b', 1), ('d', 4),
+         ('c', 2), ('g', 2), ('b', 0), ('d', 3), ('c', 1), ('g', 1), ('e', 5), ('d', 2), ('c', 0), ('g', 0), ('e', 4),
+         ('d', 1), ('e', 3), ('d', 0), ('e', 2), ('e', 1), ('e', 0))
 
 NT = (((1,), (1,)), ((), ()))
 TN = (((0,), (0,)), ((), ()))
@@ -71,39 +77,56 @@
     for d in range(1, n_dev):
         pl.semaphore_signal(barrier, inc=1, device_id=((me + d) % n_dev,), device_id_type=MESH)
 
-    idx_copy.wait()
     ones = jnp.ones((8, tok), jnp.bfloat16)
     row_id = lax.broadcasted_iota(jnp.int32, (8, 2 * n_exp), 0)
     e_id = lax.broadcasted_iota(jnp.int32, (n_exp, tok), 0)
-    cnt = jnp.zeros((8, 2 * n_exp), jnp.float32)
-    for r in range(n_lay // 2):
-        hots = []
-        for h in range(2):
-            ids = idx_v[2 * r + h]
-            acc = jnp.zeros((n_exp, tok), jnp.float32)
-            for k in range(top_k):
-                acc = jnp.where(e_id == ids[k:k + 1], 1.0, acc)
-            hots.append(acc.astype(jnp.bfloat16))
-        both = jnp.concatenate(hots, axis=0)
-        res = lax.dot_general(ones, both, NT, preferred_element_type=jnp.float32)
-        cnt = jnp.where(row_id == r, res, cnt)
-    cnt_src[...] = cnt
-    cnt_in[me] = cnt
+
+    def count_rows(part_no, r0, r1):
+        cnt = jnp.zeros((8, 2 * n_exp), jnp.float32)
+        for r in range(r0, r1):
+            hots = []
+            for h in range(2):
+                ids = idx_v[2 * r + h]
+                acc = jnp.zeros((n_exp, tok), jnp.float32)
+                for k in range(top_k):
+                    acc = jnp.where(e_id == ids[k:k + 1], 1.0, acc)
+                hots.append(acc.astype(jnp.bfloat16))
+            both = jnp.concatenate(hots, axis=0)
+            res = lax.dot_general(ones, both, NT, preferred_element_type=jnp.float32)
+            cnt = jnp.where(row_id == r, res, cnt)
+        cnt_src[part_no] = cnt
+        cnt_in[part_no, me] = cnt
+
+    def cnt_copy(p, to, frm):
+        return pltpu.make_async_remote_copy(
+            src_ref=cnt_src.at[p], dst_ref=cnt_in.at[p, frm], send_sem=cs_sem.at[p, to], recv_sem=cr_sem.at[p, frm],
+            device_id=(to,), device_id_type=MESH)
+
+    def send_counts(p):
+        for d in range(1, n_dev):
+            cnt_copy(p, (me + d) % n_dev, me).start()
+
+    def take_counts(p, lo, hi):
+        for d in range(1, n_dev):
+            cnt_copy(p, (me + d) % n_dev, (me + d) % n_dev).wait_recv()
+        tot = cnt_in[p, 0]
+        for j in range(1, n_dev):
+            tot = tot + cnt_in[p, j]
+        cols = jnp.transpose(tot * pull)
+        for i in range(lo, hi):
+            o = (i % 2) * n_exp
+            fcol[i] = jnp.broadcast_to(cols[o:o + n_exp, i // 2:i // 2 + 1], (n_exp, fcol.shape[2]))
+
+    idx_copy.wait()
+    count_rows(0, 0, 1)
     loss_acc[...] = jnp.zeros_like(loss_acc)
     pl.semaphore_wait(barrier, n_dev - 1)
-
-    def cnt_copy(to, frm):
-        return pltpu.make_async_remote_copy(
-            src_ref=cnt_src, dst_ref=cnt_in.at[frm], send_sem=cs_sem.at[to], recv_sem=cr_sem.at[frm],
-            device_id=(to,), device_id_type=MESH)
+    send_counts(0)
 
     def loss_copy(to, frm):
         return pltpu.make_async_remote_copy(
             src_ref=loss_src, dst_ref=loss_in.at[frm], send_sem=ls_sem.at[to], recv_sem=lr_sem.at[frm],
             device_id=(to,), device_id_type=MESH)
-
-    for d in range(1, n_dev):
-        cnt_copy((me + d) % n_dev, me).start()
 
     def rcopy(stage, src, dst, m, dev):
         return pltpu.make_async_remote_copy(
@@ -187,7 +210,7 @@
             lg_v[:, lo:lo + lanes] = lax.dot_general(
                 wv[lay], ubuf[lay % NU, lo:lo + lanes, :], NT, preferred_element_type=jnp.float32)
 
-    def g_part(lay, h, keep):
+    def g_part(lay, to, h, keep):
         lo = h * lanes
         logits = lg_v[:, lo:lo + lanes]
         ids = idx_v[lay, :, lo:lo + lanes]
@@ -207,101 +230,111 @@
             g = g + jnp.where(e_half == ids[k:k + 1], dch[k:k + 1], 0.0)
         main = gate * slots + jnp.where(first, pf_sum * (1.0 / tok_all), 0.0)
         total = loss_acc[:, lo:lo + lanes] + main
-        loss_acc[:, lo:lo + lanes] = total if keep is None else jnp.where(keep, total, 0.0)
-        gout[lay, :, lo:lo + lanes] = g.astype(jnp.bfloat16)
-
-    def p_part(lay):
+        loss_acc[:, lo:lo + lanes] = total if keep is None else jnp.where(keep, total, loss_acc[:, lo:lo + lanes])
+        gout[to, :, lo:lo + lanes] = g.astype(jnp.bfloat16)
+
+    def p_part(lay, to):
         dim = ubuf.shape[2]
         for h in range(2):
             lo = h * (dim // 2)
-            pg = jnp.dot(gout[lay], ubuf[lay % NU, :, lo:lo + dim // 2], preferred_element_type=jnp.float32)
-            part[lay, :, :, lo:lo + dim // 2] = pg.reshape(part.shape[1:3] + (dim // 2,))
-
-    slot_v[...] = jnp.zeros_like(slot_v)
-    lg_v[...] = jnp.zeros_like(lg_v)
-    fcol[0] = jnp.zeros(fcol.shape[1:], jnp.float32)
-
-    @pl.loop(0, n_lay)
+            pg = jnp.dot(gout[to], ubuf[lay % NU, :, lo:lo + dim // 2], preferred_element_type=jnp.float32)
+            part[to, :, :, lo:lo + dim // 2] = pg.reshape(part.shape[1:3] + (dim // 2,))
+
+    def refill(lay, c):
+        @pl.when(lay + 2 < n_lay)
+        def _():
+            e_copy(lay + 2, c, (lay % 2) * NC + c).start()
+
+    def fetch(lay):
+        @pl.when(lay + 2 < n_lay)
+        def _():
+            w_copy(lay + 2).start()
+            u_copy(lay + 2).start()
+            d_copy(lay + 2).start()
+
+    run = {'a': do_a, 'b': do_b, 'c': do_c, 'g': do_ag1, 'd': do_d, 'e': do_e}
+
+    w_copy(0).wait()
+    u_copy(0).wait()
+    d_copy(0).wait()
+    for c in range(NC):
+        e_copy(0, c, c).wait()
+        slot_chunk(0, c, c)
+        if c == 0:
+            logit_part(0)
+        e_copy(2, c, c).start()
+    w_copy(2).start()
+    u_copy(2).start()
+    d_copy(2).start()
+    take_counts(0, 0, 2)
+    for h in range(2):
+        g_part(0, 0, h, None)
+    p_part(0, 0)
+    c_pair(0).start()
+    count_rows(1, 1, n_lay // 2)
+    send_counts(1)
+
+    @pl.loop(1, n_lay)
     def _(lay):
         base = (lay % 2) * NC
-        prev = jnp.maximum(lay - 1, 0)
-        keep = lay >= 1
-
-        def refill(c):
-            @pl.when(lay + 2 < n_lay)
-            def _():
-                e_copy(lay + 2, c, base + c).start()
-
-        @pl.when(lay >= 2)
-        def _():
-            do_a(lay - 2)
-
+        prev = lay - 1
+        to = jnp.where(lay == 1, lay, prev)
+        keep = lay >= 2
+
+        def comm(c):
+            for k in 'abcgde':
+                if FIRST[k][1] == c:
+                    @pl.when(lay == FIRST[k][0])
+                    def _(k=k):
+                        run[k](0)
+                if LAG[k][1] == c:
+                    lag = LAG[k][0]
+                    hi = min(n_lay, lag + AGL) if k in 'gde' else n_lay
+
+                    @pl.when(jnp.logical_and(lay > lag, lay < hi))
+                    def _(k=k, lag=lag):
+                        run[k](lay - lag)
+
+        comm(0)
         w_copy(lay).wait()
         u_copy(lay).wait()
         d_copy(lay).wait()
         e_copy(lay, 0, base).wait()
         slot_chunk(lay, 0, base)
-        g_part(prev, 0, keep)
-        refill(0)
-
-        @pl.when(lay >= 3)
-        def _():
-            do_b(lay - 3)
-
+        g_part(prev, to, 0, keep)
+        refill(lay, 0)
+
+        comm(1)
         e_copy(lay, 1, base + 1).wait()
         slot_chunk(lay, 1, base + 1)
-        g_part(prev, 1, keep)
-        refill(1)
-
-        @pl.when(lay >= 4)
-        def _():
-            do_c(lay - 4)
-            do_ag1(lay - 4)
-
+        g_part(prev, to, 1, keep)
+        refill(lay, 1)
+
+        comm(2)
         e_copy(lay, 2, base + 2).wait()
         slot_chunk(lay, 2, base + 2)
-        p_part(prev)
-        refill(2)
-
-        @pl.when(lay + 2 < n_lay)
-        def _():
-            w_copy(lay + 2).start()
-            u_copy(lay + 2).start()
-            d_copy(lay + 2).start()
-
-        @pl.when(lay >= 1)
+        p_part(prev, to)
+        refill(lay, 2)
+        fetch(lay)
+
+        @pl.when(lay >= 2)
         def _():
             c_pair(lay - 1).start()
 
-        @pl.when(lay >= 5)
-        def _():
-            do_d(lay - 5)
-
+        comm(3)
         e_copy(lay, 3, base + 3).wait()
         slot_chunk(lay, 3, base + 3)
         logit_part(lay)
-        refill(3)
-
-        @pl.when(lay >= 6)
+        refill(lay, 3)
+
+        @pl.when(lay == 2)
         def _():
-            do_e(lay - 6)
-
-        @pl.when(lay == 0)
-        def _():
-            for d in range(1, n_dev):
-                cnt_copy((me + d) % n_dev, (me + d) % n_dev).wait_recv()
-            tot = cnt_in[0]
-            for j in range(1, n_dev):
-                tot = tot + cnt_in[j]
-            cols = jnp.transpose(tot * pull)
-            for i in range(n_lay):
-                o = (i % 2) * n_exp
-                fcol[i] = jnp.broadcast_to(cols[o:o + n_exp, i // 2:i // 2 + 1], (n_exp, fcol.shape[2]))
+            take_counts(1, 2, n_lay)
 
     last = n_lay - 1
     for h in range(2):
-        g_part(last, h, None)
-    p_part(last)
+        g_part(last, last, h, None)
+    p_part(last, last)
     la = loss_acc[...]
     lv = la[:, :128]
     for j in range(1, tok // 128):
@@ -310,19 +343,10 @@
     loss_in[me] = lv
     c_pair(last).start()
 
-    def do_cg(m):
-        do_c(m)
-        do_ag1(m)
-
-    steps = (do_a, do_b, do_cg, do_d, do_e)
-    for r in range(6):
-        for j in range(5):
-            m = last - 1 + r - j
-            if m <= last and j >= r - 1:
-                steps[j](m)
-        if r == 0:
-            for d in range(1, n_dev):
-                loss_copy((me + d) % n_dev, me).start()
+    for d in range(1, n_dev):
+        loss_copy((me + d) % n_dev, me).start()
+    for k, back in DRAIN:
+        run[k](last - back)
 
     for d in range(1, n_dev):
         loss_copy((me + d) % n_dev, (me + d) % n_dev).wait_recv()
@@ -331,7 +355,8 @@
         tot = tot + loss_in[j]
     loss_out[...] = tot
     for d in range(1, n_dev):
-        cnt_copy((me + d) % n_dev, me).wait_send()
+        cnt_copy(0, (me + d) % n_dev, me).wait_send()
+        cnt_copy(1, (me + d) % n_dev, me).wait_send()
         loss_copy((me + d) % n_dev, me).wait_send()
 
     @pl.loop(0, n_lay)
@@ -355,6 +380,9 @@
     @pl.loop(0, n_lay)
     def _(lay):
         put_f(lay).start()
+
+    @pl.loop(0, n_lay)
+    def _(lay):
         dn = lax.dot_general(g_v[lay], w_v[lay], TN, preferred_element_type=jnp.float32)
         stage[lay] = dn.astype(jnp.bfloat16)
         put(lay).start()
@@ -404,8 +432,8 @@
                 pltpu.VMEM((n_lay, pieces // 2, prow, dim), f32),
                 pltpu.VMEM((n_lay, pieces // 4, prow, dim), f32),
                 pltpu.VMEM((n_lay, pieces // 8, prow, dim), f32),
-                pltpu.VMEM((8, 128), f32),
-                pltpu.VMEM((n_dev, 8, 128), f32),
+                pltpu.VMEM((2, 8, 128), f32),
+                pltpu.VMEM((2, n_dev, 8, 128), f32),
                 pltpu.VMEM((8, 128), f32),
                 pltpu.VMEM((n_dev, 8, 128), f32),
                 pltpu.VMEM((n_lay, n_exp, 128), f32),
@@ -413,7 +441,7 @@
                 pltpu.VMEM((n_exp, tok), f32),
                 pltpu.VMEM((top_k, tok), f32),
                 dma, dma((NB,)), dma((NU,)), dma((NU,)), dma((n_lay,)),
-                dma((n_dev,)), dma((n_dev,)), dma((n_dev,)), dma((n_dev,)),
+                dma((2, n_dev)), dma((2, n_dev)), dma((n_dev,)), dma((n_dev,)),
                 dma((6, n_lay)), dma((6, n_lay)),
             ],
             compiler_params=pltpu.CompilerParams(

time: 109 us -> 107 us (0.982)
  Pallas kernels: 108 us -> 106 us
    pallas_call x1, Pallas kernels: 98.4 us -> 96.9 us  [local_step(): pl.pallas_call(lambda *refs: step_kernel(n_lay, n_dev, tok_all, *refs), o...]
where the time goes in v4:
time: 107 us
  Pallas kernels  106 us (99%)
    pallas_call x1, Pallas kernels, local_step(): pl.pallas_call(lambda *refs: step_kernel(n_lay, n_dev, tok_all, *refs), o...  96.9 us
    pallas_call x1, Pallas kernels, local_step(): pl.pallas_call(lambda *refs: out_kernel(n_lay, *refs), out_shape=(jax.Sha...  9.18 us

profile of v4, /device:TPU:0, one launch (start us, length us, event | category | flops | bytes accessed | tf_op | source)
XLA Modules:
  0.0 106.7 jit_solution(7103044175441366011)
XLA Ops:
  0.6 96.9 %router_step.1 = (f32[16,8,8,2048]{3,2,1,0:T(8,128)S(1)}, bf16[16,64,256]{2,1,0:T(8,128)(2,1)S(1)}, bf16[16,64,2048]{2,1,0:T(8,128)(2,1)S(1)}, f32[8,128]{1,0:T(8,128)S(1)}) custom-call(s32[16,8,256]{2,1,0:T(8,128)} %bitcast.8, bf16[16,2048,2048]{2,1,0:T(8,128)(2,1)} %bitcast.1.refs_1_, bf16[16,256,2048]{2,1,0:T(8,128)(2,1)} %refs_2_.1, ...), custom_call_target="tpu_custom_call" | custom-call | tf_op jit(solution)/shard_map/router_step/pallas_call | solution.py:416
  97.5 9.2 %router_out.1 = (bf16[16,256,2048]{2,1,0:T(8,128)(2,1)}, f32[16,8,8,2048]{3,2,1,0:T(8,128)}, f32[1,1]{1,0:T(1,128)}) custom-call(bf16[16,64,256]{2,1,0:T(8,128)(2,1)S(1)} %get-tuple-element.10.refs_0_, bf16[16,64,2048]{2,1,0:T(8,128)(2,1)S(1)} %get-tuple-element.11.refs_1_, f32[16,8,8,2048]{3,2,1,0:T(8,128)S(1)} %get-tuple-element.12.refs_2_, ...), custom_call_target="tpu_custom_call" | custom-call | tf_op jit(solution)/shard_map/router_out/pallas_call | solution.py:451

commit v5 on v4

--- a/solution.py
+++ b/solution.py
@@ -8,7 +8,7 @@
 AUX_COEF = 0.02
 MESH = pl.DeviceIdType.MESH
 
-NB = 8
+NB = 4
 NC = 4
 NU = 3
 AGL = 10
@@ -61,17 +61,14 @@
 
     idx_copy = pltpu.make_async_copy(idx_hbm, idx_v, idx_sem)
     idx_copy.start()
-    for c in range(2):
-        if c == 0:
-            w_copy(0).start()
-            u_copy(0).start()
-            d_copy(0).start()
-        else:
-            w_copy(1).start()
-            u_copy(1).start()
-            d_copy(1).start()
-        for j in range(NC):
-            e_copy(c, j, c * NC + j).start()
+    w_copy(0).start()
+    u_copy(0).start()
+    d_copy(0).start()
+    for j in range(NC):
+        e_copy(0, j, j).start()
+    w_copy(1).start()
+    u_copy(1).start()
+    d_copy(1).start()
 
     barrier = pltpu.get_barrier_semaphore()
     for d in range(1, n_dev):
@@ -241,9 +238,9 @@
             part[to, :, :, lo:lo + dim // 2] = pg.reshape(part.shape[1:3] + (dim // 2,))
 
     def refill(lay, c):
-        @pl.when(lay + 2 < n_lay)
+        @pl.when(lay + 1 < n_lay)
         def _():
-            e_copy(lay + 2, c, (lay % 2) * NC + c).start()
+            e_copy(lay + 1, c, c).start()
 
     def fetch(lay):
         @pl.when(lay + 2 < n_lay)
@@ -262,7 +259,7 @@
         slot_chunk(0, c, c)
         if c == 0:
             logit_part(0)
-        e_copy(2, c, c).start()
+        e_copy(1, c, c).start()
     w_copy(2).start()
     u_copy(2).start()
     d_copy(2).start()
@@ -276,7 +273,7 @@
 
     @pl.loop(1, n_lay)
     def _(lay):
-        base = (lay % 2) * NC
+        base = 0
         prev = lay - 1
         to = jnp.where(lay == 1, lay, prev)
         keep = lay >= 2

time: 107 us -> 104 us (0.972)
  Pallas kernels: 106 us -> 104 us
    pallas_call x1, Pallas kernels: 96.9 us -> 94.4 us  [local_step(): pl.pallas_call(lambda *refs: step_kernel(n_lay, n_dev, tok_all, *refs), o...]
where the time goes in v5:
time: 104 us
  Pallas kernels  104 us (100%)
    pallas_call x1, Pallas kernels, local_step(): pl.pallas_call(lambda *refs: step_kernel(n_lay, n_dev, tok_all, *refs), o...  94.4 us
    pallas_call x1, Pallas kernels, local_step(): pl.pallas_call(lambda *refs: out_kernel(n_lay, *refs), out_shape=(jax.Sha...  9.18 us

profile of v5, /device:TPU:0, one launch (start us, length us, event | category | flops | bytes accessed | tf_op | source)
XLA Modules:
  0.0 104.3 jit_solution(3792789081289755566)
XLA Ops:
  0.6 94.4 %router_step.1 = (f32[16,8,8,2048]{3,2,1,0:T(8,128)S(1)}, bf16[16,64,256]{2,1,0:T(8,128)(2,1)S(1)}, bf16[16,64,2048]{2,1,0:T(8,128)(2,1)S(1)}, f32[8,128]{1,0:T(8,128)S(1)}) custom-call(s32[16,8,256]{2,1,0:T(8,128)} %bitcast.8, bf16[16,2048,2048]{2,1,0:T(8,128)(2,1)} %bitcast.1.refs_1_, bf16[16,256,2048]{2,1,0:T(8,128)(2,1)} %refs_2_.1, ...), custom_call_target="tpu_custom_call" | custom-call | tf_op jit(solution)/shard_map/router_step/pallas_call | solution.py:413
  95.1 9.2 %router_out.1 = (bf16[16,256,2048]{2,1,0:T(8,128)(2,1)}, f32[16,8,8,2048]{3,2,1,0:T(8,128)}, f32[1,1]{1,0:T(1,128)}) custom-call(bf16[16,64,256]{2,1,0:T(8,128)(2,1)S(1)} %get-tuple-element.10.refs_0_, bf16[16,64,2048]{2,1,0:T(8,128)(2,1)S(1)} %get-tuple-element.11.refs_1_, f32[16,8,8,2048]{3,2,1,0:T(8,128)S(1)} %get-tuple-element.12.refs_2_, ...), custom_call_target="tpu_custom_call" | custom-call | tf_op jit(solution)/shard_map/router_out/pallas_call | solution.py:448

commit v6 on v5

--- a/solution.py
+++ b/solution.py
@@ -8,9 +8,9 @@
 AUX_COEF = 0.02
 MESH = pl.DeviceIdType.MESH
 
-NB = 4
+NB = 3
 NC = 4
-NU = 3
+NU = 4
 AGL = 10
 LAG = {'a': (2, 1), 'b': (3, 3), 'c': (4, 3), 'g': (4, 3), 'd': (6, 0), 'e': (7, 3)}
 FIRST = {'a': (1, 2), 'b': (2, 3), 'c': (3, 3), 'g': (3, 3), 'd': (4, 3), 'e': (6, 1)}
@@ -64,7 +64,7 @@
     w_copy(0).start()
     u_copy(0).start()
     d_copy(0).start()
-    for j in range(NC):
+    for j in range(NB):
         e_copy(0, j, j).start()
     w_copy(1).start()
     u_copy(1).start()
@@ -237,17 +237,20 @@
             pg = jnp.dot(gout[to], ubuf[lay % NU, :, lo:lo + dim // 2], preferred_element_type=jnp.float32)
             part[to, :, :, lo:lo + dim // 2] = pg.reshape(part.shape[1:3] + (dim // 2,))
 
+    def slot_of(lay, c):
+        return (lay * NC + c) % NB
+
     def refill(lay, c):
-        @pl.when(lay + 1 < n_lay)
+        dl, dc = (c + NB) // NC, (c + NB) % NC
+
+        @pl.when(lay + dl < n_lay)
         def _():
-            e_copy(lay + 1, c, c).start()
-
-    def fetch(lay):
+            e_copy(lay + dl, dc, slot_of(lay, c)).start()
+
+    def fetch(copy, lay):
         @pl.when(lay + 2 < n_lay)
         def _():
-            w_copy(lay + 2).start()
-            u_copy(lay + 2).start()
-            d_copy(lay + 2).start()
+            copy(lay + 2).start()
 
     run = {'a': do_a, 'b': do_b, 'c': do_c, 'g': do_ag1, 'd': do_d, 'e': do_e}
 
@@ -255,11 +258,12 @@
     u_copy(0).wait()
     d_copy(0).wait()
     for c in range(NC):
-        e_copy(0, c, c).wait()
-        slot_chunk(0, c, c)
+        e_copy(0, c, slot_of(0, c)).wait()
+        slot_chunk(0, c, slot_of(0, c))
         if c == 0:
             logit_part(0)
-        e_copy(1, c, c).start()
+        dl, dc = (c + NB) // NC, (c + NB) % NC
+        e_copy(dl, dc, slot_of(0, c)).start()
     w_copy(2).start()
     u_copy(2).start()
     d_copy(2).start()
@@ -273,7 +277,6 @@
 
     @pl.loop(1, n_lay)
     def _(lay):
-        base = 0
         prev = lay - 1
         to = jnp.where(lay == 1, lay, prev)
         keep = lay >= 2
@@ -296,31 +299,33 @@
         w_copy(lay).wait()
         u_copy(lay).wait()
         d_copy(lay).wait()
-        e_copy(lay, 0, base).wait()
-        slot_chunk(lay, 0, base)
+        e_copy(lay, 0, slot_of(lay, 0)).wait()
+        slot_chunk(lay, 0, slot_of(lay, 0))
         g_part(prev, to, 0, keep)
         refill(lay, 0)
+        fetch(d_copy, lay)
 
         comm(1)
-        e_copy(lay, 1, base + 1).wait()
-        slot_chunk(lay, 1, base + 1)
+        e_copy(lay, 1, slot_of(lay, 1)).wait()
+        slot_chunk(lay, 1, slot_of(lay, 1))
         g_part(prev, to, 1, keep)
         refill(lay, 1)
+        fetch(u_copy, lay)
 
         comm(2)
-        e_copy(lay, 2, base + 2).wait()
-        slot_chunk(lay, 2, base + 2)
+        e_copy(lay, 2, slot_of(lay, 2)).wait()
+        slot_chunk(lay, 2, slot_of(lay, 2))
         p_part(prev, to)
         refill(lay, 2)
-        fetch(lay)
+        fetch(w_copy, lay)
 
         @pl.when(lay >= 2)
         def _():
             c_pair(lay - 1).start()
 
         comm(3)
-        e_copy(lay, 3, base + 3).wait()
-        slot_chunk(lay, 3, base + 3)
+        e_copy(lay, 3, slot_of(lay, 3)).wait()
+        slot_chunk(lay, 3, slot_of(lay, 3))
         logit_part(lay)
         refill(lay, 3)
 

time: 104 us -> 104 us (level)
  no operation moved by 1% of the time
where the time goes in v6:
time: 104 us
  Pallas kernels  103 us (99%)
    pallas_call x1, Pallas kernels, local_step(): pl.pallas_call(lambda *refs: step_kernel(n_lay, n_dev, tok_all, *refs), o...  94 us
    pallas_call x1, Pallas kernels, local_step(): pl.pallas_call(lambda *refs: out_kernel(n_lay, *refs), out_shape=(jax.Sha...  9.18 us

profile of v6, /device:TPU:0, one launch (start us, length us, event | category | flops | bytes accessed | tf_op | source)
XLA Modules:
  0.0 103.9 jit_solution(15336385768873576355)
XLA Ops:
  0.6 94.0 %router_step.1 = (f32[16,8,8,2048]{3,2,1,0:T(8,128)S(1)}, bf16[16,64,256]{2,1,0:T(8,128)(2,1)S(1)}, bf16[16,64,2048]{2,1,0:T(8,128)(2,1)S(1)}, f32[8,128]{1,0:T(8,128)S(1)}) custom-call(s32[16,8,256]{2,1,0:T(8,128)} %bitcast.8, bf16[16,2048,2048]{2,1,0:T(8,128)(2,1)} %bitcast.1.refs_1_, bf16[16,256,2048]{2,1,0:T(8,128)(2,1)} %refs_2_.1, ...), custom_call_target="tpu_custom_call" | custom-call | tf_op jit(solution)/shard_map/router_step/pallas_call | solution.py:418
  94.7 9.2 %router_out.1 = (bf16[16,256,2048]{2,1,0:T(8,128)(2,1)}, f32[16,8,8,2048]{3,2,1,0:T(8,128)}, f32[1,1]{1,0:T(1,128)}) custom-call(bf16[16,64,256]{2,1,0:T(8,128)(2,1)S(1)} %get-tuple-element.10.refs_0_, bf16[16,64,2048]{2,1,0:T(8,128)(2,1)S(1)} %get-tuple-element.11.refs_1_, f32[16,8,8,2048]{3,2,1,0:T(8,128)S(1)} %get-tuple-element.12.refs_2_, ...), custom_call_target="tpu_custom_call" | custom-call | tf_op jit(solution)/shard_map/router_out/pallas_call | solution.py:453

commit v7 on v6

--- a/solution.py
+++ b/solution.py
@@ -11,12 +11,13 @@
 NB = 3
 NC = 4
 NU = 4
-AGL = 10
-LAG = {'a': (2, 1), 'b': (3, 3), 'c': (4, 3), 'g': (4, 3), 'd': (6, 0), 'e': (7, 3)}
-FIRST = {'a': (1, 2), 'b': (2, 3), 'c': (3, 3), 'g': (3, 3), 'd': (4, 3), 'e': (6, 1)}
-DRAIN = (('a', 1), ('g', 5), ('e', 6), ('g', 4), ('a', 0), ('b', 2), ('c', 3), ('g', 3), ('d', 5), ('b', 1), ('d', 4),
-         ('c', 2), ('g', 2), ('b', 0), ('d', 3), ('c', 1), ('g', 1), ('e', 5), ('d', 2), ('c', 0), ('g', 0), ('e', 4),
-         ('d', 1), ('e', 3), ('d', 0), ('e', 2), ('e', 1), ('e', 0))
+AGL = 12
+LAG = {'a': (2, 1), 'b': (3, 3), 'c': (4, 3), 'g': (4, 3), 'd': (6, 0), 'e': (8, 1)}
+FIRST = {'a': (1, 1), 'b': (2, 3), 'c': (3, 3), 'g': (3, 3), 'd': (5, 0), 'e': (6, 2)}
+DRAIN = (('a', 1), ('d', 5), ('e', 7), ('e', 6), ('a', 0), ('b', 2), ('c', 3), ('d', 4), ('b', 1), ('g', 3), ('c', 2),
+         ('e', 5), ('g', 2), ('b', 0), ('c', 1), ('g', 1), ('d', 3), ('e', 4), ('d', 2), ('x', 0), ('c', 0), ('g', 0), ('d', 1),
+         ('e', 3), ('y', 0), ('d', 0), ('e', 2), ('e', 1), ('e', 0))
+OLD = 9
 
 NT = (((1,), (1,)), ((), ()))
 TN = (((0,), (0,)), ((), ()))
@@ -117,8 +118,6 @@
     idx_copy.wait()
     count_rows(0, 0, 1)
     loss_acc[...] = jnp.zeros_like(loss_acc)
-    pl.semaphore_wait(barrier, n_dev - 1)
-    send_counts(0)
 
     def loss_copy(to, frm):
         return pltpu.make_async_remote_copy(
@@ -261,6 +260,8 @@
         e_copy(0, c, slot_of(0, c)).wait()
         slot_chunk(0, c, slot_of(0, c))
         if c == 0:
+            pl.semaphore_wait(barrier, n_dev - 1)
+            send_counts(0)
             logit_part(0)
         dl, dc = (c + NB) // NC, (c + NB) % NC
         e_copy(dl, dc, slot_of(0, c)).start()
@@ -347,29 +348,42 @@
 
     for d in range(1, n_dev):
         loss_copy((me + d) % n_dev, me).start()
+    def sent(lo, hi):
+        @pl.loop(lo, hi)
+        def _(m):
+            c_pair(m).wait_send()
+            c_rs1(m).wait_send()
+            c_rs2(m).wait_send()
+            c_ag1(m, mine).wait_send()
+            c_ag2(m, quart).wait_send()
+
+    def whole(lo, hi):
+        @pl.loop(lo, hi)
+        def _(m):
+            do_f(m)
+            c_out(m, half).wait_send()
+
+    def old(_):
+        sent(0, OLD)
+        whole(0, OLD)
+
+    def take_loss(_):
+        for d in range(1, n_dev):
+            loss_copy((me + d) % n_dev, (me + d) % n_dev).wait_recv()
+        tot = loss_in[0]
+        for j in range(1, n_dev):
+            tot = tot + loss_in[j]
+        loss_out[...] = tot
+        for d in range(1, n_dev):
+            cnt_copy(0, (me + d) % n_dev, me).wait_send()
+            cnt_copy(1, (me + d) % n_dev, me).wait_send()
+            loss_copy((me + d) % n_dev, me).wait_send()
+
+    run['x'], run['y'] = old, take_loss
     for k, back in DRAIN:
         run[k](last - back)
-
-    for d in range(1, n_dev):
-        loss_copy((me + d) % n_dev, (me + d) % n_dev).wait_recv()
-    tot = loss_in[0]
-    for j in range(1, n_dev):
-        tot = tot + loss_in[j]
-    loss_out[...] = tot
-    for d in range(1, n_dev):
-        cnt_copy(0, (me + d) % n_dev, me).wait_send()
-        cnt_copy(1, (me + d) % n_dev, me).wait_send()
-        loss_copy((me + d) % n_dev, me).wait_send()
-
-    @pl.loop(0, n_lay)
-    def _(m):
-        do_f(m)
-        c_pair(m).wait_send()
-        c_rs1(m).wait_send()
-        c_rs2(m).wait_send()
-        c_ag1(m, mine).wait_send()
-        c_ag2(m, quart).wait_send()
-        c_out(m, half).wait_send()
+    sent(OLD, n_lay)
+    whole(OLD, n_lay)
 
 
 def out_kernel(n_lay, g_v, w_v, f_v, l_v, dn_hbm, dr_hbm, loss, stage, st_sem, f_sem):

time: 104 us -> 105 us (level)
  Pallas kernels: 103 us -> 105 us
    pallas_call x1, Pallas kernels: 94 us -> 95.4 us  [local_step(): pl.pallas_call(lambda *refs: step_kernel(n_lay, n_dev, tok_all, *refs), o...]
where the time goes in v7:
time: 105 us
  Pallas kernels  105 us (100%)
    pallas_call x1, Pallas kernels, local_step(): pl.pallas_call(lambda *refs: step_kernel(n_lay, n_dev, tok_all, *refs), o...  95.4 us
    pallas_call x1, Pallas kernels, local_step(): pl.pallas_call(lambda *refs: out_kernel(n_lay, *refs), out_shape=(jax.Sha...  9.18 us

profile of v7, /device:TPU:0, one launch (start us, length us, event | category | flops | bytes accessed | tf_op | source)
XLA Modules:
  0.0 105.2 jit_solution(11523327308010353735)
XLA Ops:
  0.6 95.4 %router_step.1 = (f32[16,8,8,2048]{3,2,1,0:T(8,128)S(1)}, bf16[16,64,256]{2,1,0:T(8,128)(2,1)S(1)}, bf16[16,64,2048]{2,1,0:T(8,128)(2,1)S(1)}, f32[8,128]{1,0:T(8,128)S(1)}) custom-call(s32[16,8,256]{2,1,0:T(8,128)} %bitcast.8, bf16[16,2048,2048]{2,1,0:T(8,128)(2,1)} %bitcast.1.refs_1_, bf16[16,256,2048]{2,1,0:T(8,128)(2,1)} %refs_2_.1, ...), custom_call_target="tpu_custom_call" | custom-call | tf_op jit(solution)/shard_map/router_step/pallas_call | solution.py:432
  96.0 9.2 %router_out.1 = (bf16[16,256,2048]{2,1,0:T(8,128)(2,1)}, f32[16,8,8,2048]{3,2,1,0:T(8,128)}, f32[1,1]{1,0:T(1,128)}) custom-call(bf16[16,64,256]{2,1,0:T(8,128)(2,1)S(1)} %get-tuple-element.10.refs_0_, bf16[16,64,2048]{2,1,0:T(8,128)(2,1)S(1)} %get-tuple-element.11.refs_1_, f32[16,8,8,2048]{3,2,1,0:T(8,128)S(1)} %get-tuple-element.12.refs_2_, ...), custom_call_target="tpu_custom_call" | custom-call | tf_op jit(solution)/shard_map/router_out/pallas_call | solution.py:467

commit v8 on v7

--- a/solution.py
+++ b/solution.py
@@ -11,12 +11,12 @@
 NB = 3
 NC = 4
 NU = 4
-AGL = 12
-LAG = {'a': (2, 1), 'b': (3, 3), 'c': (4, 3), 'g': (4, 3), 'd': (6, 0), 'e': (8, 1)}
-FIRST = {'a': (1, 1), 'b': (2, 3), 'c': (3, 3), 'g': (3, 3), 'd': (5, 0), 'e': (6, 2)}
-DRAIN = (('a', 1), ('d', 5), ('e', 7), ('e', 6), ('a', 0), ('b', 2), ('c', 3), ('d', 4), ('b', 1), ('g', 3), ('c', 2),
-         ('e', 5), ('g', 2), ('b', 0), ('c', 1), ('g', 1), ('d', 3), ('e', 4), ('d', 2), ('x', 0), ('c', 0), ('g', 0), ('d', 1),
-         ('e', 3), ('y', 0), ('d', 0), ('e', 2), ('e', 1), ('e', 0))
+AGL = 10
+LAG = {'a': (2, 1), 'b': (3, 3), 'c': (4, 3), 'g': (4, 3), 'd': (6, 0), 'e': (7, 3)}
+FIRST = {'a': (1, 2), 'b': (2, 3), 'c': (3, 3), 'g': (3, 3), 'd': (4, 3), 'e': (6, 1)}
+DRAIN = (('a', 1), ('g', 5), ('e', 6), ('g', 4), ('a', 0), ('b', 2), ('c', 3), ('g', 3), ('d', 5), ('b', 1), ('d', 4),
+         ('c', 2), ('g', 2), ('b', 0), ('d', 3), ('c', 1), ('g', 1), ('e', 5), ('d', 2), ('x', 0), ('c', 0), ('g', 0), ('e', 4),
+         ('d', 1), ('e', 3), ('y', 0), ('d', 0), ('e', 2), ('e', 1), ('e', 0))
 OLD = 9
 
 NT = (((1,), (1,)), ((), ()))
@@ -118,6 +118,8 @@
     idx_copy.wait()
     count_rows(0, 0, 1)
     loss_acc[...] = jnp.zeros_like(loss_acc)
+    pl.semaphore_wait(barrier, n_dev - 1)
+    send_counts(0)
 
     def loss_copy(to, frm):
         return pltpu.make_async_remote_copy(
@@ -260,8 +262,6 @@
         e_copy(0, c, slot_of(0, c)).wait()
         slot_chunk(0, c, slot_of(0, c))
         if c == 0:
-            pl.semaphore_wait(barrier, n_dev - 1)
-            send_counts(0)
             logit_part(0)
         dl, dc = (c + NB) // NC, (c + NB) % NC
         e_copy(dl, dc, slot_of(0, c)).start()

time: 105 us -> 104 us (level)
  Pallas kernels: 105 us -> 103 us
    pallas_call x1, Pallas kernels: 95.4 us -> 94 us  [local_step(): pl.pallas_call(lambda *refs: step_kernel(n_lay, n_dev, tok_all, *refs), o...]
where the time goes in v8:
time: 104 us
  Pallas kernels  103 us (99%)
    pallas_call x1, Pallas kernels, local_step(): pl.pallas_call(lambda *refs: step_kernel(n_lay, n_dev, tok_all, *refs), o...  94 us
    pallas_call x1, Pallas kernels, local_step(): pl.pallas_call(lambda *refs: out_kernel(n_lay, *refs), out_shape=(jax.Sha...  9.18 us

profile of v8, /device:TPU:0, one launch (start us, length us, event | category | flops | bytes accessed | tf_op | source)
XLA Modules:
  0.0 103.9 jit_solution(9594365828033642739)
XLA Ops:
  0.6 94.0 %router_step.1 = (f32[16,8,8,2048]{3,2,1,0:T(8,128)S(1)}, bf16[16,64,256]{2,1,0:T(8,128)(2,1)S(1)}, bf16[16,64,2048]{2,1,0:T(8,128)(2,1)S(1)}, f32[8,128]{1,0:T(8,128)S(1)}) custom-call(s32[16,8,256]{2,1,0:T(8,128)} %bitcast.8, bf16[16,2048,2048]{2,1,0:T(8,128)(2,1)} %bitcast.1.refs_1_, bf16[16,256,2048]{2,1,0:T(8,128)(2,1)} %refs_2_.1, ...), custom_call_target="tpu_custom_call" | custom-call | tf_op jit(solution)/shard_map/router_step/pallas_call | solution.py:432
  94.7 9.2 %router_out.1 = (bf16[16,256,2048]{2,1,0:T(8,128)(2,1)}, f32[16,8,8,2048]{3,2,1,0:T(8,128)}, f32[1,1]{1,0:T(1,128)}) custom-call(bf16[16,64,256]{2,1,0:T(8,128)(2,1)S(1)} %get-tuple-element.10.refs_0_, bf16[16,64,2048]{2,1,0:T(8,128)(2,1)S(1)} %get-tuple-element.11.refs_1_, f32[16,8,8,2048]{3,2,1,0:T(8,128)S(1)} %get-tuple-element.12.refs_2_, ...), custom_call_target="tpu_custom_call" | custom-call | tf_op jit(solution)/shard_map/router_out/pallas_call | solution.py:467

commit v9 on v8

--- a/solution.py
+++ b/solution.py
@@ -62,14 +62,16 @@
 
     idx_copy = pltpu.make_async_copy(idx_hbm, idx_v, idx_sem)
     idx_copy.start()
+    d_copy(0).start()
+    e_copy(0, 0, 0).start()
+    e_copy(0, 1, 1).start()
     w_copy(0).start()
     u_copy(0).start()
-    d_copy(0).start()
-    for j in range(NB):
+    for j in range(2, NB):
         e_copy(0, j, j).start()
+    d_copy(1).start()
     w_copy(1).start()
     u_copy(1).start()
-    d_copy(1).start()
 
     barrier = pltpu.get_barrier_semaphore()
     for d in range(1, n_dev):
@@ -116,7 +118,7 @@
             fcol[i] = jnp.broadcast_to(cols[o:o + n_exp, i // 2:i // 2 + 1], (n_exp, fcol.shape[2]))
 
     idx_copy.wait()
-    count_rows(0, 0, 1)
+    count_rows(0, 0, 2)
     loss_acc[...] = jnp.zeros_like(loss_acc)
     pl.semaphore_wait(barrier, n_dev - 1)
     send_counts(0)
@@ -255,27 +257,24 @@
 
     run = {'a': do_a, 'b': do_b, 'c': do_c, 'g': do_ag1, 'd': do_d, 'e': do_e}
 
-    w_copy(0).wait()
-    u_copy(0).wait()
     d_copy(0).wait()
     for c in range(NC):
         e_copy(0, c, slot_of(0, c)).wait()
         slot_chunk(0, c, slot_of(0, c))
-        if c == 0:
+        if c == NC - 1:
+            w_copy(0).wait()
+            u_copy(0).wait()
             logit_part(0)
         dl, dc = (c + NB) // NC, (c + NB) % NC
         e_copy(dl, dc, slot_of(0, c)).start()
     w_copy(2).start()
     u_copy(2).start()
     d_copy(2).start()
-    take_counts(0, 0, 2)
+    take_counts(0, 0, 4)
     for h in range(2):
         g_part(0, 0, h, None)
     p_part(0, 0)
     c_pair(0).start()
-    count_rows(1, 1, n_lay // 2)
-    send_counts(1)
-
     @pl.loop(1, n_lay)
     def _(lay):
         prev = lay - 1
@@ -332,7 +331,12 @@
 
         @pl.when(lay == 2)
         def _():
-            take_counts(1, 2, n_lay)
+            count_rows(1, 2, n_lay // 2)
+            send_counts(1)
+
+        @pl.when(lay == 4)
+        def _():
+            take_counts(1, 4, n_lay)
 
     last = n_lay - 1
     for h in range(2):

time: 104 us -> 104 us (level)
  no operation moved by 1% of the time
where the time goes in v9:
time: 104 us
  Pallas kernels  103 us (99%)
    pallas_call x1, Pallas kernels, local_step(): pl.pallas_call(lambda *refs: step_kernel(n_lay, n_dev, tok_all, *refs), o...  93.9 us
    pallas_call x1, Pallas kernels, local_step(): pl.pallas_call(lambda *refs: out_kernel(n_lay, *refs), out_shape=(jax.Sha...  9.17 us

profile of v9, /device:TPU:0, one launch (start us, length us, event | category | flops | bytes accessed | tf_op | source)
XLA Modules:
  0.0 103.7 jit_solution(6656734457719808776)
XLA Ops:
  0.6 93.9 %router_step.1 = (f32[16,8,8,2048]{3,2,1,0:T(8,128)S(1)}, bf16[16,64,256]{2,1,0:T(8,128)(2,1)S(1)}, bf16[16,64,2048]{2,1,0:T(8,128)(2,1)S(1)}, f32[8,128]{1,0:T(8,128)S(1)}) custom-call(s32[16,8,256]{2,1,0:T(8,128)} %bitcast.8, bf16[16,2048,2048]{2,1,0:T(8,128)(2,1)} %bitcast.1.refs_1_, bf16[16,256,2048]{2,1,0:T(8,128)(2,1)} %refs_2_.1, ...), custom_call_target="tpu_custom_call" | custom-call | tf_op jit(solution)/shard_map/router_step/pallas_call | solution.py:436
  94.5 9.2 %router_out.1 = (bf16[16,256,2048]{2,1,0:T(8,128)(2,1)}, f32[16,8,8,2048]{3,2,1,0:T(8,128)}, f32[1,1]{1,0:T(1,128)}) custom-call(bf16[16,64,256]{2,1,0:T(8,128)(2,1)S(1)} %get-tuple-element.10.refs_0_, bf16[16,64,2048]{2,1,0:T(8,128)(2,1)S(1)} %get-tuple-element.11.refs_1_, f32[16,8,8,2048]{3,2,1,0:T(8,128)S(1)} %get-tuple-element.12.refs_2_, ...), custom_call_target="tpu_custom_call" | custom-call | tf_op jit(solution)/shard_map/router_out/pallas_call | solution.py:471

commit v10 on v9

--- a/solution.py
+++ b/solution.py
@@ -11,12 +11,12 @@
 NB = 3
 NC = 4
 NU = 4
-AGL = 10
-LAG = {'a': (2, 1), 'b': (3, 3), 'c': (4, 3), 'g': (4, 3), 'd': (6, 0), 'e': (7, 3)}
-FIRST = {'a': (1, 2), 'b': (2, 3), 'c': (3, 3), 'g': (3, 3), 'd': (4, 3), 'e': (6, 1)}
-DRAIN = (('a', 1), ('g', 5), ('e', 6), ('g', 4), ('a', 0), ('b', 2), ('c', 3), ('g', 3), ('d', 5), ('b', 1), ('d', 4),
-         ('c', 2), ('g', 2), ('b', 0), ('d', 3), ('c', 1), ('g', 1), ('e', 5), ('d', 2), ('x', 0), ('c', 0), ('g', 0), ('e', 4),
-         ('d', 1), ('e', 3), ('y', 0), ('d', 0), ('e', 2), ('e', 1), ('e', 0))
+AGL = 12
+LAG = {'a': (2, 1), 'b': (3, 3), 'c': (4, 3), 'g': (4, 3), 'd': (6, 0), 'e': (8, 1)}
+FIRST = {'a': (1, 1), 'b': (2, 3), 'c': (3, 3), 'g': (3, 3), 'd': (5, 0), 'e': (6, 2)}
+DRAIN = (('a', 1), ('d', 5), ('e', 7), ('e', 6), ('a', 0), ('b', 2), ('c', 3), ('d', 4), ('b', 1), ('g', 3), ('c', 2),
+         ('e', 5), ('g', 2), ('b', 0), ('c', 1), ('g', 1), ('d', 3), ('e', 4), ('d', 2), ('x', 0), ('c', 0), ('g', 0), ('d', 1),
+         ('e', 3), ('y', 0), ('d', 0), ('e', 2), ('e', 1), ('e', 0))
 OLD = 9
 
 NT = (((1,), (1,)), ((), ()))

time: 104 us -> 105 us (level)
  no operation moved by 1% of the time
where the time goes in v10:
time: 105 us
  Pallas kernels  104 us (99%)
    pallas_call x1, Pallas kernels, local_step(): pl.pallas_call(lambda *refs: step_kernel(n_lay, n_dev, tok_all, *refs), o...  94.8 us
    pallas_call x1, Pallas kernels, local_step(): pl.pallas_call(lambda *refs: out_kernel(n_lay, *refs), out_shape=(jax.Sha...  9.18 us

profile of v10, /device:TPU:0, one launch (start us, length us, event | category | flops | bytes accessed | tf_op | source)
XLA Modules:
  0.0 104.6 jit_solution(1534965493078361948)
XLA Ops:
  0.6 94.8 %router_step.1 = (f32[16,8,8,2048]{3,2,1,0:T(8,128)S(1)}, bf16[16,64,256]{2,1,0:T(8,128)(2,1)S(1)}, bf16[16,64,2048]{2,1,0:T(8,128)(2,1)S(1)}, f32[8,128]{1,0:T(8,128)S(1)}) custom-call(s32[16,8,256]{2,1,0:T(8,128)} %bitcast.8, bf16[16,2048,2048]{2,1,0:T(8,128)(2,1)} %bitcast.1.refs_1_, bf16[16,256,2048]{2,1,0:T(8,128)(2,1)} %refs_2_.1, ...), custom_call_target="tpu_custom_call" | custom-call | tf_op jit(solution)/shard_map/router_step/pallas_call | solution.py:436
  95.5 9.2 %router_out.1 = (bf16[16,256,2048]{2,1,0:T(8,128)(2,1)}, f32[16,8,8,2048]{3,2,1,0:T(8,128)}, f32[1,1]{1,0:T(1,128)}) custom-call(bf16[16,64,256]{2,1,0:T(8,128)(2,1)S(1)} %get-tuple-element.10.refs_0_, bf16[16,64,2048]{2,1,0:T(8,128)(2,1)S(1)} %get-tuple-element.11.refs_1_, f32[16,8,8,2048]{3,2,1,0:T(8,128)S(1)} %get-tuple-element.12.refs_2_, ...), custom_call_target="tpu_custom_call" | custom-call | tf_op jit(solution)/shard_map/router_out/pallas_call | solution.py:471
